TPU v7x, 16 devices: a whole 2x2x2 slice. The times are simulated.
16 devices in a mesh: my: 4 (over z, y), mx: 4 (over x, core).
Axes of the slice: x: 2, y: 2, z: 2, core: 2. Of those that a mesh axis runs over, the one named last changes fastest.
Arguments:
- x_in: bfloat16 [512, 3584], P(None, 'mx')
- seq_lens: int32 [512], P('mx')
- gain_attn: bfloat16 [3584], P('mx')
- gain_mlp: bfloat16 [3584], P('mx')
- w_q: bfloat16 [3584, 3584], P('mx', 'my')
- b_q: bfloat16 [3584], P('my')
- w_k: bfloat16 [3584, 512], P('mx', 'my')
- b_k: bfloat16 [512], P('my')
- w_v: bfloat16 [3584, 512], P('mx', 'my')
- b_v: bfloat16 [512], P('my')
- w_o: bfloat16 [3584, 3584], P('my', 'mx')
- w_gate: bfloat16 [3584, 18944], P('mx', 'my')
- w_up: bfloat16 [3584, 18944], P('mx', 'my')
- w_down: bfloat16 [18944, 3584], P('my', 'mx')
- k_cache: bfloat16 [512, 512, 4, 128], P('mx', None, 'my')
- v_cache: bfloat16 [512, 512, 4, 128], P('mx', None, 'my')
Outputs:
- output 1: bfloat16 [512, 3584], P(None, 'mx')
- output 2: bfloat16 [512, 512, 4, 128], P('mx', None, 'my')
- output 3: bfloat16 [512, 512, 4, 128], P('mx', None, 'my')
All inputs are finite; a program needn't handle non-finite values.
Results may differ from a plain program's by a relative error of at most 0.0170983.
Values are sent between devices in bfloat16 or wider.
A program may use at most 1 GiB of HBM per device.

v0:
```python
import jax
import jax.numpy as jnp
from jax import lax
from jax.sharding import PartitionSpec as P

HEAD = 128
NORM_EPS = 1e-6
ROPE_THETA = 1000000.0


def apply_rotary(vectors, positions):
    half_dim = HEAD // 2
    inv_freq = ROPE_THETA ** (-2.0 * jnp.arange(half_dim, dtype=jnp.float32) / HEAD)
    angles = positions.astype(jnp.float32)[:, None, None] * inv_freq
    cos_tab = jnp.cos(angles)
    sin_tab = jnp.sin(angles)
    lower_half = vectors[..., :half_dim]
    upper_half = vectors[..., half_dim:]
    return jnp.concatenate([lower_half * cos_tab - upper_half * sin_tab, upper_half * cos_tab + lower_half * sin_tab], axis=-1)


def attend_local(q_rot, k_cache_out, v_cache_out, seq_lens):
    row_count, seq_len, kv_heads, _ = k_cache_out.shape
    q_heads = q_rot.shape[1]
    q_grouped = q_rot.reshape(row_count, kv_heads, q_heads // kv_heads, HEAD)
    scores = jnp.einsum("bkgd,bskd->bkgs", q_grouped, k_cache_out, preferred_element_type=jnp.float32) * HEAD ** -0.5
    visible = (jnp.arange(seq_len)[None, :] <= seq_lens[:, None])[:, None, None, :]
    scores = jnp.where(visible, scores, -jnp.inf)
    weights = jnp.exp(scores - jnp.max(scores, axis=-1, keepdims=True))
    weight_sum = jnp.sum(weights, axis=-1, keepdims=True)
    weighted = jnp.einsum("bkgs,bskd->bkgd", weights.astype(jnp.bfloat16), v_cache_out, preferred_element_type=jnp.float32)
    return (weighted / weight_sum).astype(jnp.bfloat16).reshape(row_count, q_heads * HEAD)


def solution(mesh):
    mx_size = mesh.shape["mx"]
    act_spec = P(None, "mx")
    cache_spec = P("mx", None, "my", None)
    in_specs = (act_spec, P("mx"), P("mx"), P("mx"), P("mx", "my"), P("my"), P("mx", "my"), P("my"), P("mx", "my"), P("my"), P("my", "mx"), P("mx", "my"), P("mx", "my"), P("my", "mx"), cache_spec, cache_spec)
    out_specs = (act_spec, cache_spec, cache_spec)

    def local_layer(x_in, seq_lens, gain_attn, gain_mlp, w_q, b_q, w_k, b_k, w_v, b_v, w_o, w_gate, w_up, w_down, k_cache, v_cache):
        hidden = x_in.shape[1] * mx_size
        x_f32 = x_in.astype(jnp.float32)
        attn_sq = lax.psum(jnp.sum(x_f32 * x_f32, axis=1, keepdims=True), "mx")
        normed = (x_f32 * lax.rsqrt(attn_sq / hidden + NORM_EPS) * gain_attn.astype(jnp.float32)).astype(jnp.bfloat16)
        q_cols = w_q.shape[1]
        kv_cols = w_k.shape[1]
        partials = jnp.concatenate([
            jnp.dot(normed, w_q, preferred_element_type=jnp.float32).astype(jnp.bfloat16),
            jnp.dot(normed, w_k, preferred_element_type=jnp.float32).astype(jnp.bfloat16),
            jnp.dot(normed, w_v, preferred_element_type=jnp.float32).astype(jnp.bfloat16),
        ], axis=1)
        projected = lax.psum_scatter(partials, "mx", scatter_dimension=0, tiled=True).astype(jnp.float32)
        row_count = projected.shape[0]
        kv_heads = kv_cols // HEAD
        q_vals = projected[:, :q_cols] + b_q.astype(jnp.float32)
        k_vals = projected[:, q_cols:q_cols + kv_cols] + b_k.astype(jnp.float32)
        v_vals = projected[:, q_cols + kv_cols:] + b_v.astype(jnp.float32)
        q_rot = apply_rotary(q_vals.reshape(row_count, q_cols // HEAD, HEAD), seq_lens).astype(jnp.bfloat16)
        k_rot = apply_rotary(k_vals.reshape(row_count, kv_heads, HEAD), seq_lens).astype(jnp.bfloat16)
        v_new = v_vals.reshape(row_count, kv_heads, HEAD).astype(jnp.bfloat16)
        at_slot = (jnp.arange(k_cache.shape[1])[None, :] == seq_lens[:, None])[:, :, None, None]
        k_cache_out = jnp.where(at_slot, k_rot[:, None], k_cache)
        v_cache_out = jnp.where(at_slot, v_new[:, None], v_cache)
        attn_rows = attend_local(q_rot, k_cache_out, v_cache_out, seq_lens)
        attn_all = lax.all_gather(attn_rows, "mx", axis=0, tiled=True)
        attn_proj = lax.psum(jnp.dot(attn_all, w_o, preferred_element_type=jnp.float32).astype(jnp.bfloat16), "my")
        x_mid = (x_f32 + attn_proj.astype(jnp.float32)).astype(jnp.bfloat16)
        mid_f32 = x_mid.astype(jnp.float32)
        mlp_sq = lax.psum(jnp.sum(mid_f32 * mid_f32, axis=1, keepdims=True), "mx")
        normed_mlp = (mid_f32 * lax.rsqrt(mlp_sq / hidden + NORM_EPS) * gain_mlp.astype(jnp.float32)).astype(jnp.bfloat16)
        ff_cols = w_gate.shape[1]
        gate_up = lax.psum(jnp.concatenate([
            jnp.dot(normed_mlp, w_gate, preferred_element_type=jnp.float32).astype(jnp.bfloat16),
            jnp.dot(normed_mlp, w_up, preferred_element_type=jnp.float32).astype(jnp.bfloat16),
        ], axis=1), "mx").astype(jnp.float32)
        hidden_act = (jax.nn.silu(gate_up[:, :ff_cols]) * gate_up[:, ff_cols:]).astype(jnp.bfloat16)
        down_proj = lax.psum(jnp.dot(hidden_act, w_down, preferred_element_type=jnp.float32).astype(jnp.bfloat16), "my")
        x_out = (mid_f32 + down_proj.astype(jnp.float32)).astype(jnp.bfloat16)
        return x_out, k_cache_out, v_cache_out

    return jax.shard_map(local_layer, mesh=mesh, in_specs=in_specs, out_specs=out_specs, check_vma=False)
```

profile of v0, /device:TPU:0, one launch (start us, length us, event | category | flops | bytes accessed | tf_op | source)
XLA Modules:
  0.0 425.0 jit_solution(18118893701971442687)
XLA Ops:
  7.2 1.6 fusion.8
  8.8 8.6 %psum.35 = f32[512,1]{0,1:T(1,128)S(1)} all-reduce(f32[512,1]{0,1:T(1,128)S(1)} %bitcast.35), channel_id=1, replica_groups=mesh['my'=4,'mx'=4] {'mx'}, use_global_device_ids=true, to_apply=%region_1.0 | all-reduce | flops 512 | bytes 4096 | tf_op jit(solution)/shard_map/psum | solution.py:45
  18.2 1.7 convolution_convert_fusion.5
  20.3 1.3 convolution_convert_fusion.3
  21.7 1.1 pad_maximum_fusion.1
  23.4 21.4 %reduce-scatter.2.cloned.1.call-done = bf16[128,1152]{1,0:T(8,128)(2,1)} async-done(((bf16[512,1152]{1,0:T(8,128)(2,1)}), bf16[128,1152]{1,0:T(8,128)(2,1)}) %reduce-scatter.2.cloned.1.call-update) | async-done | bytes 294928 | tf_op jit(solution)/shard_map/reduce_scatter | solution.py:54
  44.8 1.0 convert_element_type.101
  47.2 23.3 %broadcast_select_fusion.1 = (bf16[128,512,1,128]{3,1,2,0:T(8,128)(2,1)}, bf16[128,512,1,128]{3,1,2,0:T(8,128)(2,1)}) fusion(bf16[128,512,1,128]{3,1,2,0:T(8,128)(2,1)} %param.30, pred[128,512]{1,0:T(8,128)(4,1)S(1)} %get-tuple-element.18, bf16[128,128]{1,0:T(8,128)(2,1)S(1)} %pad_maximum_fusion.2, bf16[128,512,1,128]{3,1,2,0:T(8,128)(2,1)} %param.31, ...), kind=kLoop, calls=%fused_computation.5 | loop fusion | flops 16777216 | bytes 67239936 | tf_op jit(solution)/shard_map/jit(_where)/select_n | solution.py:64
  70.5 11.6 %fusion.7 = (f32[128,7]{1,0:T(8,128)S(1)}, f32[128,7,512]{2,1,0:T(8,128)}) fusion(pred[128,512]{1,0:T(8,128)(4,1)S(1)} %get-tuple-element.17, bf16[128,512,1,128]{3,1,2,0:T(8,128)(2,1)} %get-tuple-element.13, bf16[128,7,64]{2,1,0:T(8,128)(2,1)S(1)} %get-tuple-element.6, bf16[128,7,64]{2,1,0:T(8,128)(2,1)S(1)} %get-tuple-element.5), kind=kOutput, calls=%fused_computation.20 | convolution fusion | flops 119274624 | bytes 18910720 | tf_op jit(solution)/shard_map/bkgd,bskd->bkgs/dot_general | solution.py:26
  82.1 2.5 fusion.16
  84.6 7.3 %fusion.24 = bf16[128,7,128]{2,1,0:T(8,128)(2,1)S(1)} fusion(bf16[128,512,1,128]{3,1,2,0:T(8,128)(2,1)} %get-tuple-element.14, f32[128,7,512]{2,1,0:T(8,128)S(1)} %copy-done.2, f32[128,7]{1,0:T(8,128)S(1)} %get-tuple-element.19, pred[128,512]{1,0:T(8,128)(4,1)S(1)} %get-tuple-element.17, f32[128,7]{1,0:T(8,128)S(1)} %fusion.16), kind=kOutput, calls=%fused_computation.35 | convolution fusion | flops 119504896 | bytes 18914304 | tf_op jit(solution)/shard_map/bkgs,bskd->bkgd/dot_general | solution.py:31
  92.1 8.8 %all_gather.3 = bf16[512,896]{0,1:T(8,128)(2,1)S(1)} all-gather(bf16[128,896]{0,1:T(8,128)(2,1)S(1)} %bitcast.33), channel_id=1, replica_groups=mesh['my'=4,'mx'=4] {'mx'}, dimensions={0}, use_global_device_ids=true | all-gather | bytes 1146880 | tf_op jit(solution)/shard_map/all_gather | solution.py:67
  100.9 3.6 convolution_convert_fusion.2
  104.6 43.2 %all-reduce.4.cloned.1.call-done = bf16[512,896]{1,0:T(8,128)(2,1)} async-done(((bf16[512,896]{1,0:T(8,128)(2,1)}), bf16[512,896]{1,0:T(8,128)(2,1)}) %all-reduce.4.cloned.1.call-update) | async-done | bytes 917520 | tf_op jit(solution)/shard_map/psum | solution.py:68
  147.8 1.6 fusion.12
  149.4 6.6 %psum.37 = f32[512,1]{0,1:T(1,128)S(1)} all-reduce(f32[512,1]{0,1:T(1,128)S(1)} %bitcast.34), channel_id=1, replica_groups=mesh['my'=4,'mx'=4] {'mx'}, use_global_device_ids=true, to_apply=%region_7.8 | all-reduce | flops 512 | bytes 4096 | tf_op jit(solution)/shard_map/psum | solution.py:71
  156.0 9.1 %convolution_convert_fusion = bf16[512,4736]{1,0:T(8,128)(2,1)S(1)} fusion(bf16[896,4736]{1,0:T(8,128)(2,1)} %param.28, bf16[512,896]{1,0:T(8,128)(2,1)S(1)} %get-tuple-element.4, f32[896]{0:T(1024)S(1)} %convert_element_type.113, f32[512]{0:T(512)S(1)} %bitcast.39), kind=kOutput, calls=%fused_computation.9 | convolution fusion | flops 4349558784 | bytes 14259712 | tf_op jit(solution)/shard_map/dot_general | solution.py:76
  165.1 9.1 %convolution_convert_fusion.1 = bf16[512,4736]{1,0:T(8,128)(2,1)S(1)} fusion(bf16[896,4736]{1,0:T(8,128)(2,1)} %param.27, bf16[512,896]{1,0:T(8,128)(2,1)S(1)} %get-tuple-element.4, f32[896]{0:T(1024)S(1)} %convert_element_type.113, f32[512]{0:T(512)S(1)} %bitcast.40), kind=kOutput, calls=%fused_computation.10 | convolution fusion | flops 4349558784 | bytes 14259712 | tf_op jit(solution)/shard_map/dot_general | solution.py:75
  174.3 4.8 %pad_maximum_fusion = bf16[512,9472]{1,0:T(8,128)(2,1)} fusion(bf16[512,4736]{1,0:T(8,128)(2,1)S(1)} %convolution_convert_fusion, bf16[512,4736]{1,0:T(8,128)(2,1)S(1)} %convolution_convert_fusion.1), kind=kLoop, calls=%fused_computation.8 | loop fusion | flops 19398656 | bytes 19398656 | tf_op jit(solution)/shard_map/concatenate | solution.py:74
  179.2 169.7 %all-reduce.6.cloned.1.call-done = bf16[512,9472]{1,0:T(8,128)(2,1)} async-done(((bf16[512,9472]{1,0:T(8,128)(2,1)}), bf16[512,9472]{1,0:T(8,128)(2,1)}) %all-reduce.6.cloned.1.call-update) | async-done | bytes 9699344 | tf_op jit(solution)/shard_map/psum | solution.py:74
  348.9 11.7 %convert_element_type.117 = f32[512,9472]{1,0:T(8,128)} convert(bf16[512,9472]{1,0:T(8,128)(2,1)} %all-reduce.6.cloned.1.call-done) | non-fusion elementwise | flops 4849664 | bytes 29097984 | tf_op jit(solution)/shard_map/convert_element_type | solution.py:77
  360.6 12.7 %fusion.18 = bf16[512,896]{1,0:T(8,128)(2,1)} fusion(bf16[4736,896]{1,0:T(8,128)(2,1)} %param.29, f32[512,9472]{1,0:T(8,128)} %convert_element_type.117), kind=kOutput, calls=%fused_computation.31 | convolution fusion | flops 4360306688 | bytes 28803072 | tf_op jit(solution)/shard_map/dot_general | solution.py:79
  373.3 42.8 %all-reduce.8.cloned.1.call-done = bf16[512,896]{1,0:T(8,128)(2,1)} async-done(((bf16[512,896]{1,0:T(8,128)(2,1)}), bf16[512,896]{1,0:T(8,128)(2,1)}) %all-reduce.8.cloned.1.call-update) | async-done | bytes 917520 | tf_op jit(solution)/shard_map/psum | solution.py:79
  416.1 2.3 fusion.15
  (50 shorter events, 3.4 us)
Async XLA Ops:
  7.2 13.2 %copy-start = (bf16[896,896]{1,0:T(8,128)(2,1)S(1)}, bf16[896,896]{1,0:T(8,128)(2,1)}, u32[]{:S(2)}) copy-start(bf16[896,896]{1,0:T(8,128)(2,1)} %param.20) | copy-start | bytes 4816900
  7.2 12.7 %copy-start.3 = (bf16[512,896]{1,0:T(8,128)(2,1)S(1)}, bf16[512,896]{1,0:T(8,128)(2,1)}, u32[]{:S(2)}) copy-start(bf16[512,896]{1,0:T(8,128)(2,1)} %param.16) | copy-start | bytes 2752516
  7.2 12.7 %copy-start.7 = (bf16[896,128]{1,0:T(8,128)(2,1)S(1)}, bf16[896,128]{1,0:T(8,128)(2,1)}, u32[]{:S(2)}) copy-start(bf16[896,128]{1,0:T(8,128)(2,1)} %param.24) | copy-start | bytes 688132
  7.2 37.6 %reduce-scatter.2.cloned.1.call-start = ((), (), s32[]{:S(2)}) async-start(), calls=%async_computation.1 | async-start | bytes 1474560 | tf_op jit(solution)/shard_map/reduce_scatter | solution.py:54
  21.6 1.2 copy-start.6
  21.6 1.3 copy-start.8
  21.6 1.3 copy-start.9
  21.6 1.3 copy-start.4
  22.8 125.0 %all-reduce.4.cloned.1.call-start = ((), (), s32[]{:S(2)}) async-start(), calls=%async_computation.2 | async-start | bytes 1835008 | tf_op jit(solution)/shard_map/psum | solution.py:68
  82.1 2.5 copy-start.2
  100.9 3.7 copy-start.5
  104.5 244.4 %all-reduce.6.cloned.1.call-start = ((), (), s32[]{:S(2)}) async-start(), calls=%async_computation.3 | async-start | bytes 19398656 | tf_op jit(solution)/shard_map/psum | solution.py:74
  179.1 237.0 %all-reduce.8.cloned.1.call-start = ((), (), s32[]{:S(2)}) async-start(), calls=%async_computation.4 | async-start | bytes 1835008 | tf_op jit(solution)/shard_map/psum | solution.py:79
  360.6 57.8 %copy-start.1 = (bf16[896,896]{1,0:T(8,128)(2,1)S(1)}, bf16[896,896]{1,0:T(8,128)(2,1)}, u32[]{:S(2)}) copy-start(bf16[896,896]{1,0:T(8,128)(2,1)} %param.20) | copy-start | bytes 4816900
Sparse Core Ops, SparseCore 0:
  22.9 21.8 reduce-scatter.1
  104.7 43.1 all-reduce.3
  179.2 169.6 all-reduce.5
  373.4 42.6 all-reduce.7
where the time goes:
time: 425 us
  waiting for transfers between devices  277 us (65%)
  matrix products  56.8 us (13%)
  other arithmetic  51.7 us (12%)
  blocking collectives  24 us (6%)
  between operations  14.1 us (3%)
    psum x1, waiting for transfers between devices, local_layer(): lax.psum(jnp.concatenate([jnp.dot(normed_mlp, w_gate, preferred_element_t...  170 us
    psum x1, waiting for transfers between devices, local_layer(): lax.psum(jnp.dot(attn_all, w_o, preferred_element_type=jnp.float32).astyp...  43.2 us
    psum x1, waiting for transfers between devices, local_layer(): lax.psum(jnp.dot(hidden_act, w_down, preferred_element_type=jnp.float32)....  42.8 us
    select_n x1, other arithmetic, local_layer(): k_cache_out = jnp.where(at_slot, k_rot[:, None], k_cache)  23.3 us
    reduce_scatter x1, waiting for transfers between devices, local_layer(): lax.psum_scatter(partials, 'mx', scatter_dimension=0, tiled=True)  21.4 us
    dot_general x1, matrix products, local_layer(): jnp.dot(hidden_act, w_down, preferred_element_type=jnp.float32)  12.7 us
    convert_element_type x1, other arithmetic, local_layer(): gate_up = lax.psum(jnp.concatenate([jnp.dot(normed_mlp, w_gate, preferred...  11.7 us
    dot_general x1, matrix products, attend_local(): jnp.einsum('bkgd,bskd->bkgs', q_grouped, k_cache_out, preferred_element_t...  11.6 us
  transfers between devices with their start and end apart: 4, of which 4 were waited for; matrix products, arithmetic and copies ran while one was open for 0% of the time, Pallas kernels for 0%

commit v1 on v0

--- a/solution.py
+++ b/solution.py
@@ -1,11 +1,302 @@
 import jax
 import jax.numpy as jnp
 from jax import lax
+from jax.experimental import pallas as pl
+from jax.experimental.pallas import tpu as pltpu
 from jax.sharding import PartitionSpec as P
 
 HEAD = 128
 NORM_EPS = 1e-6
 ROPE_THETA = 1000000.0
+CHUNKS = 4
+MESH_IDS = pl.DeviceIdType.MESH
+
+
+def over_tiles(total, tile, body):
+    count = total // tile
+
+    def step(i, carry):
+        body(pl.multiple_of(i * tile, tile), tile)
+        return carry
+
+    lax.fori_loop(0, count, step, 0)
+    if total % tile:
+        body(count * tile, total % tile)
+
+
+def mx_peers():
+    me = lax.axis_index("mx")
+    core = lax.rem(me, 2)
+    sib = me + 1 - 2 * core
+    return me, sib, lax.rem(me + 2, 4), lax.rem(sib + 2, 4)
+
+
+def my_peers():
+    me = lax.axis_index("my")
+    flip = me + 1 - 2 * lax.rem(me, 2)
+    return me, (flip, lax.rem(me + 2, 4), lax.rem(flip + 2, 4))
+
+
+def column_to_lanes(col):
+    rows = col.shape[0]
+    return jnp.transpose(jnp.broadcast_to(col, (rows, rows)))[:8]
+
+
+def lanes_to_column(lanes):
+    width = lanes.shape[1]
+    return jnp.transpose(jnp.broadcast_to(lanes[:1], (width, width)))
+
+
+def enter(axis_peers):
+    barrier = pltpu.get_barrier_semaphore()
+    for axis, peer in axis_peers:
+        pl.semaphore_signal(barrier, inc=1, device_id={axis: peer}, device_id_type=MESH_IDS)
+    pl.semaphore_wait(barrier, len(axis_peers))
+
+
+def mlp_kernel(attn, x_in, gain, w_o, w_gate, w_up, w_down, out,
+               wo_v, wg_v, wu_v, wd_v, x_v, attn_all, o_part, o_recv, mid, stat_send, stat_recv, h2,
+               part, pair_recv, cross_send, cross_recv, act, acc, d_part, d_recv, out_all,
+               w_sem, s_gather, r_gather, s_red, r_red, s_bc, r_bc, s_stat, r_stat, s_pair, r_pair,
+               s_cross, r_cross, s_act, r_act, s_red2, r_red2, s_bc2, r_bc2, out_sem):
+    mx, sib, across, across_sib = mx_peers()
+    my, my_list = my_peers()
+    rb = mid.shape[2]
+    hid = mid.shape[3]
+    ff = wg_v.shape[1]
+    rows = 4 * rb
+
+    def remote(src, dst, send, recv, axis, peer):
+        return pltpu.make_async_remote_copy(src_ref=src, dst_ref=dst, send_sem=send, recv_sem=recv, device_id={axis: peer}, device_id_type=MESH_IDS)
+
+    loads = [
+        pltpu.make_async_copy(w_o, wo_v, w_sem.at[0]),
+        pltpu.make_async_copy(x_in.at[pl.ds(pl.multiple_of(my * CHUNKS * rb, CHUNKS * rb), CHUNKS * rb)], x_v, w_sem.at[1]),
+        pltpu.make_async_copy(w_gate, wg_v, w_sem.at[2]),
+        pltpu.make_async_copy(w_up, wu_v, w_sem.at[3]),
+        pltpu.make_async_copy(w_down, wd_v, w_sem.at[4]),
+    ]
+    for load in loads:
+        load.start()
+    enter([("mx", sib), ("mx", across), ("mx", across_sib)] + [("my", p) for p in my_list])
+
+    def gather_copies(k):
+        src = attn.at[pl.ds(k * rb, rb)]
+        return (remote(src, attn_all.at[k, mx], s_gather.at[k, 0], r_gather.at[k, 0], "mx", across),
+                remote(src, attn_all.at[k, mx], s_gather.at[k, 1], r_gather.at[k, 1], "mx", sib),
+                remote(attn_all.at[k, across], attn_all.at[k, across], s_gather.at[k, 2], r_gather.at[k, 2], "mx", sib))
+
+    def reduce_copies(k, src, dst, send, recv):
+        return [remote(src.at[k, p], dst.at[k, d], send.at[k, d], recv.at[k, d], "my", p) for d, p in enumerate(my_list)]
+
+    def bcast_copies(k, buf, send, recv):
+        return [remote(buf.at[k, my], buf.at[k, my], send.at[k, d], recv.at[k, d], "my", p) for d, p in enumerate(my_list)]
+
+    def stat_copies(k):
+        return [remote(stat_send.at[k], stat_recv.at[k, d], s_stat.at[k, d], r_stat.at[k, d], "mx", p) for d, p in enumerate((sib, across, across_sib))]
+
+    def pair_copies(k):
+        return [remote(part.at[k, across_sib], pair_recv.at[k, 0], s_pair.at[k, 0], r_pair.at[k, 0], "mx", sib),
+                remote(part.at[k, sib], pair_recv.at[k, 1], s_pair.at[k, 1], r_pair.at[k, 1], "mx", sib)]
+
+    def cross_copy(k):
+        return remote(cross_send.at[k], cross_recv.at[k], s_cross.at[k], r_cross.at[k], "mx", across)
+
+    def act_copies(k):
+        return (remote(act.at[k, mx], act.at[k, mx], s_act.at[k, 0], r_act.at[k, 0], "mx", across),
+                remote(act.at[k, mx], act.at[k, mx], s_act.at[k, 1], r_act.at[k, 1], "mx", sib),
+                remote(act.at[k, across], act.at[k, across], s_act.at[k, 2], r_act.at[k, 2], "mx", sib))
+
+    def start_gather(k):
+        to_across, to_sib, _ = gather_copies(k)
+        to_across.start()
+        to_sib.start()
+        attn_all[k, mx] = attn[pl.ds(k * rb, rb), :]
+
+    def forward_gather(k):
+        to_across, _, forward = gather_copies(k)
+        to_across.wait_recv()
+        forward.start()
+
+    def out_proj(k):
+        _, to_sib, forward = gather_copies(k)
+        to_sib.wait_recv()
+        forward.wait_recv()
+        if k == 0:
+            loads[0].wait()
+        rows_in = attn_all[k].reshape(rows, hid)
+        o_part[k] = jnp.dot(rows_in, wo_v[...], preferred_element_type=jnp.float32).astype(jnp.bfloat16).reshape(4, rb, hid)
+        for copy in reduce_copies(k, o_part, o_recv, s_red, r_red):
+            copy.start()
+
+    def own_block(k):
+        for copy in reduce_copies(k, o_part, o_recv, s_red, r_red):
+            copy.wait_recv()
+        if k == 0:
+            loads[1].wait()
+        total = o_part[k, my].astype(jnp.float32)
+        for d in range(3):
+            total += o_recv[k, d].astype(jnp.float32)
+        mid[k, my] = (x_v[k * rb:(k + 1) * rb].astype(jnp.float32) + total).astype(jnp.bfloat16)
+        for copy in bcast_copies(k, mid, s_bc, r_bc):
+            copy.start()
+
+    def stats(k):
+        for copy in bcast_copies(k, mid, s_bc, r_bc):
+            copy.wait_recv()
+        rows_f32 = mid[k].reshape(rows, hid).astype(jnp.float32)
+        stat_send[k] = column_to_lanes(jnp.sum(rows_f32 * rows_f32, axis=1, keepdims=True))
+        for copy in stat_copies(k):
+            copy.start()
+
+    def gate_up(k):
+        for copy in stat_copies(k):
+            copy.wait_recv()
+        if k == 0:
+            loads[2].wait()
+            loads[3].wait()
+        total = stat_send[k] + stat_recv[k, 0] + stat_recv[k, 1] + stat_recv[k, 2]
+        scale = lanes_to_column(lax.rsqrt(total / (4 * hid) + NORM_EPS))
+        gain_row = gain[...].astype(jnp.float32)
+        for t in range(hid // 128):
+            cols = slice(t * 128, (t + 1) * 128)
+            piece = mid[k, :, :, cols].reshape(rows, 128).astype(jnp.float32)
+            h2[:, cols] = (piece * scale * gain_row[:, cols]).astype(jnp.bfloat16)
+
+        def body(off, tile):
+            lhs = h2[...]
+            part[k, :, :, pl.ds(off, tile)] = jnp.dot(lhs, wg_v[:, pl.ds(off, tile)], preferred_element_type=jnp.float32).astype(jnp.bfloat16).reshape(4, rb, tile)
+            part[k, :, :, pl.ds(pl.multiple_of(off + ff, 128), tile)] = jnp.dot(lhs, wu_v[:, pl.ds(off, tile)], preferred_element_type=jnp.float32).astype(jnp.bfloat16).reshape(4, rb, tile)
+
+        over_tiles(ff, 512, body)
+        for copy in pair_copies(k):
+            copy.start()
+
+    def pair_sum(k):
+        pair_copies(k)[0].wait_recv()
+
+        def body(off, tile):
+            cols = pl.ds(off, tile)
+            cross_send[k, :, cols] = (part[k, across, :, cols].astype(jnp.float32) + pair_recv[k, 0, :, cols].astype(jnp.float32)).astype(jnp.bfloat16)
+
+        over_tiles(2 * ff, 512, body)
+        cross_copy(k).start()
+
+    def activate(k):
+        pair_copies(k)[1].wait_recv()
+        cross_copy(k).wait_recv()
+
+        def total(cols):
+            return part[k, mx, :, cols].astype(jnp.float32) + pair_recv[k, 1, :, cols].astype(jnp.float32) + cross_recv[k, :, cols].astype(jnp.float32)
+
+        def body(off, tile):
+            gate = total(pl.ds(off, tile))
+            up = total(pl.ds(pl.multiple_of(off + ff, 128), tile))
+            act[k, mx, :, pl.ds(off, tile)] = (jax.nn.silu(gate) * up).astype(jnp.bfloat16)
+
+        over_tiles(ff, 512, body)
+        to_across, to_sib, _ = act_copies(k)
+        to_across.start()
+        to_sib.start()
+
+    def forward_act(k):
+        to_across, _, forward = act_copies(k)
+        to_across.wait_recv()
+        forward.start()
+
+    def down(k):
+        _, to_sib, forward = act_copies(k)
+        to_sib.wait_recv()
+        forward.wait_recv()
+        if k == 0:
+            loads[4].wait()
+        acc[...] = jnp.zeros_like(acc)
+
+        def body(off, tile):
+            lhs = act[k, :, :, pl.ds(off, tile)].reshape(rows, tile)
+            acc[...] += jnp.dot(lhs, wd_v[pl.ds(off, tile), :], preferred_element_type=jnp.float32)
+
+        over_tiles(ff, 512, body)
+        d_part[k] = acc[...].astype(jnp.bfloat16).reshape(4, rb, hid)
+        for copy in reduce_copies(k, d_part, d_recv, s_red2, r_red2):
+            copy.start()
+
+    def out_block(k):
+        for copy in reduce_copies(k, d_part, d_recv, s_red2, r_red2):
+            copy.wait_recv()
+        total = d_part[k, my].astype(jnp.float32)
+        for d in range(3):
+            total += d_recv[k, d].astype(jnp.float32)
+        out_all[k, my] = (mid[k, my].astype(jnp.float32) + total).astype(jnp.bfloat16)
+        for copy in bcast_copies(k, out_all, s_bc2, r_bc2):
+            copy.start()
+
+    def out_copies(k):
+        return [pltpu.make_async_copy(out_all.at[k, j], out.at[pl.ds((j * CHUNKS + k) * rb, rb)], out_sem.at[k, j]) for j in range(4)]
+
+    def write_out(k):
+        for copy in bcast_copies(k, out_all, s_bc2, r_bc2):
+            copy.wait_recv()
+        for copy in out_copies(k):
+            copy.start()
+
+    for k in range(CHUNKS):
+        start_gather(k)
+    plan = [(forward_gather, 0), (out_proj, 0), (forward_gather, 1), (out_proj, 1), (own_block, 0), (own_block, 1), (stats, 0),
+            (forward_gather, 2), (out_proj, 2), (gate_up, 0), (stats, 1), (pair_sum, 0), (gate_up, 1), (own_block, 2), (forward_gather, 3), (out_proj, 3),
+            (pair_sum, 1), (stats, 2), (own_block, 3), (gate_up, 2), (stats, 3), (activate, 0), (pair_sum, 2), (gate_up, 3), (activate, 1), (pair_sum, 3),
+            (forward_act, 0), (down, 0), (activate, 2), (forward_act, 1), (down, 1), (out_block, 0), (activate, 3), (out_block, 1), (write_out, 0),
+            (forward_act, 2), (down, 2), (write_out, 1), (forward_act, 3), (down, 3), (out_block, 2), (out_block, 3), (write_out, 2), (write_out, 3)]
+    for stage, k in plan:
+        stage(k)
+
+    for k in range(CHUNKS):
+        sends = list(gather_copies(k)) + reduce_copies(k, o_part, o_recv, s_red, r_red) + bcast_copies(k, mid, s_bc, r_bc) + stat_copies(k)
+        sends += pair_copies(k) + [cross_copy(k)] + list(act_copies(k))
+        sends += reduce_copies(k, d_part, d_recv, s_red2, r_red2) + bcast_copies(k, out_all, s_bc2, r_bc2)
+        for copy in sends:
+            copy.wait_send()
+        for copy in out_copies(k):
+            copy.wait()
+
+
+def mlp_call(attn, x_in, gain, w_o, w_gate, w_up, w_down):
+    row_total, hid = x_in.shape
+    ff = w_gate.shape[1]
+    rb = row_total // (4 * CHUNKS)
+    bf16 = jnp.bfloat16
+    f32 = jnp.float32
+    vmem = pl.BlockSpec(memory_space=pltpu.VMEM)
+    hbm = pl.BlockSpec(memory_space=pl.ANY)
+    dma = pltpu.SemaphoreType.DMA
+    return pl.pallas_call(
+        mlp_kernel,
+        out_shape=jax.ShapeDtypeStruct((row_total, hid), bf16),
+        in_specs=[vmem, hbm, vmem, hbm, hbm, hbm, hbm],
+        out_specs=hbm,
+        scratch_shapes=[
+            pltpu.VMEM(w_o.shape, bf16), pltpu.VMEM(w_gate.shape, bf16), pltpu.VMEM(w_up.shape, bf16), pltpu.VMEM(w_down.shape, bf16),
+            pltpu.VMEM((CHUNKS * rb, hid), bf16),
+            pltpu.VMEM((CHUNKS, 4, rb, hid), bf16),
+            pltpu.VMEM((CHUNKS, 4, rb, hid), bf16), pltpu.VMEM((CHUNKS, 3, rb, hid), bf16),
+            pltpu.VMEM((CHUNKS, 4, rb, hid), bf16),
+            pltpu.VMEM((CHUNKS, 8, 4 * rb), f32), pltpu.VMEM((CHUNKS, 3, 8, 4 * rb), f32),
+            pltpu.VMEM((4 * rb, hid), bf16),
+            pltpu.VMEM((CHUNKS, 4, rb, 2 * ff), bf16), pltpu.VMEM((CHUNKS, 2, rb, 2 * ff), bf16),
+            pltpu.VMEM((CHUNKS, rb, 2 * ff), bf16), pltpu.VMEM((CHUNKS, rb, 2 * ff), bf16),
+            pltpu.VMEM((CHUNKS, 4, rb, ff), bf16),
+            pltpu.VMEM((4 * rb, hid), f32),
+            pltpu.VMEM((CHUNKS, 4, rb, hid), bf16), pltpu.VMEM((CHUNKS, 3, rb, hid), bf16),
+            pltpu.VMEM((CHUNKS, 4, rb, hid), bf16),
+            dma((5,)),
+            dma((CHUNKS, 3)), dma((CHUNKS, 3)), dma((CHUNKS, 3)), dma((CHUNKS, 3)), dma((CHUNKS, 3)), dma((CHUNKS, 3)),
+            dma((CHUNKS, 3)), dma((CHUNKS, 3)), dma((CHUNKS, 2)), dma((CHUNKS, 2)),
+            dma((CHUNKS,)), dma((CHUNKS,)), dma((CHUNKS, 3)), dma((CHUNKS, 3)),
+            dma((CHUNKS, 3)), dma((CHUNKS, 3)), dma((CHUNKS, 3)), dma((CHUNKS, 3)), dma((CHUNKS, 4)),
+        ],
+        compiler_params=pltpu.CompilerParams(collective_id=1, has_side_effects=True, vmem_limit_bytes=67043328),
+        name="attn_out_mlp",
+    )(attn, x_in, gain.reshape(1, hid), w_o, w_gate, w_up, w_down)
 
 
 def apply_rotary(vectors, positions):
@@ -64,20 +355,7 @@
         k_cache_out = jnp.where(at_slot, k_rot[:, None], k_cache)
         v_cache_out = jnp.where(at_slot, v_new[:, None], v_cache)
         attn_rows = attend_local(q_rot, k_cache_out, v_cache_out, seq_lens)
-        attn_all = lax.all_gather(attn_rows, "mx", axis=0, tiled=True)
-        attn_proj = lax.psum(jnp.dot(attn_all, w_o, preferred_element_type=jnp.float32).astype(jnp.bfloat16), "my")
-        x_mid = (x_f32 + attn_proj.astype(jnp.float32)).astype(jnp.bfloat16)
-        mid_f32 = x_mid.astype(jnp.float32)
-        mlp_sq = lax.psum(jnp.sum(mid_f32 * mid_f32, axis=1, keepdims=True), "mx")
-        normed_mlp = (mid_f32 * lax.rsqrt(mlp_sq / hidden + NORM_EPS) * gain_mlp.astype(jnp.float32)).astype(jnp.bfloat16)
-        ff_cols = w_gate.shape[1]
-        gate_up = lax.psum(jnp.concatenate([
-            jnp.dot(normed_mlp, w_gate, preferred_element_type=jnp.float32).astype(jnp.bfloat16),
-            jnp.dot(normed_mlp, w_up, preferred_element_type=jnp.float32).astype(jnp.bfloat16),
-        ], axis=1), "mx").astype(jnp.float32)
-        hidden_act = (jax.nn.silu(gate_up[:, :ff_cols]) * gate_up[:, ff_cols:]).astype(jnp.bfloat16)
-        down_proj = lax.psum(jnp.dot(hidden_act, w_down, preferred_element_type=jnp.float32).astype(jnp.bfloat16), "my")
-        x_out = (mid_f32 + down_proj.astype(jnp.float32)).astype(jnp.bfloat16)
+        x_out = mlp_call(attn_rows, x_in, gain_mlp, w_o, w_gate, w_up, w_down)
         return x_out, k_cache_out, v_cache_out
 
     return jax.shard_map(local_layer, mesh=mesh, in_specs=in_specs, out_specs=out_specs, check_vma=False)

time: 425 us -> 229 us (0.54)
  waiting for transfers between devices: 277 us -> 20.9 us
  Pallas kernels: 0 us -> 132 us
  matrix products: 56.8 us -> 18.9 us
  other arithmetic: 51.7 us -> 29.5 us
  blocking collectives: 24 us -> 8.77 us
    psum x3 -> x0, waiting for transfers between devices: 256 us -> none  [the longest x1 170 us: local_layer(): lax.psum(jnp.concatenate([jnp.dot(normed_mlp, w_gate, preferred_element_t...]
    pallas_call x0 -> x1, Pallas kernels: none -> 132 us  [mlp_call(): pl.pallas_call(mlp_kernel, out_shape=jax.ShapeDtypeStruct((row_total, hid...]
    dot_general x4 -> x0, matrix products: 34.6 us -> none  [the longest x1 12.7 us: local_layer(): jnp.dot(hidden_act, w_down, preferred_element_type=jnp.float32)]
    convert_element_type x3 -> x0, other arithmetic: 14.1 us -> none  [the longest x1 11.7 us: local_layer(): gate_up = lax.psum(jnp.concatenate([jnp.dot(normed_mlp, w_gate, preferred...]
    all_gather x1 -> x0, blocking collectives: 8.77 us -> none  [local_layer(): attn_all = lax.all_gather(attn_rows, 'mx', axis=0, tiled=True)]
    psum x1 -> x0, blocking collectives: 6.58 us -> none  [local_layer(): mlp_sq = lax.psum(jnp.sum(mid_f32 * mid_f32, axis=1, keepdims=True), 'mx')]
    concatenate x1 -> x0, other arithmetic: 4.78 us -> none  [local_layer(): jnp.concatenate([jnp.dot(normed_mlp, w_gate, preferred_element_type=jnp.f...]
  transfers between devices with their start and end apart: 4 -> 1, of which waited for: 4 -> 1; matrix products, arithmetic and copies ran while one was open for 0% -> 0% of each run, Pallas kernels for 0% -> 0%
where the time goes in v1:
time: 229 us
  Pallas kernels  132 us (58%)
  other arithmetic  29.5 us (13%)
  waiting for transfers between devices  20.9 us (9%)
  matrix products  18.9 us (8%)
  between operations  14.3 us (6%)
  blocking collectives  8.77 us (4%)
  local copies, waits for them, and re-layouts  4.58 us (2%)
    pallas_call x1, Pallas kernels, mlp_call(): pl.pallas_call(mlp_kernel, out_shape=jax.ShapeDtypeStruct((row_total, hid...  132 us
    select_n x1, other arithmetic, local_layer(): k_cache_out = jnp.where(at_slot, k_rot[:, None], k_cache)  23.3 us
    reduce_scatter x1, waiting for transfers between devices, local_layer(): lax.psum_scatter(partials, 'mx', scatter_dimension=0, tiled=True)  20.9 us
    psum x1, blocking collectives, local_layer(): attn_sq = lax.psum(jnp.sum(x_f32 * x_f32, axis=1, keepdims=True), 'mx')  8.77 us
    dot_general x1, matrix products, attend_local(): jnp.einsum('bkgd,bskd->bkgs', q_grouped, k_cache_out, preferred_element_t...  8.17 us
    dot_general x1, matrix products, attend_local(): jnp.einsum('bkgs,bskd->bkgd', weights.astype(jnp.bfloat16), v_cache_out,...  7.28 us
  transfers between devices with their start and end apart: 1, of which 1 were waited for; matrix products, arithmetic and copies ran while one was open for 0% of the time, Pallas kernels for 0%

profile of v1, /device:TPU:0, one launch (start us, length us, event | category | flops | bytes accessed | tf_op | source)
XLA Modules:
  0.0 228.5 jit_solution(12024259182514775011)
XLA Ops:
  7.2 0.8 convert_element_type.57
  8.0 1.4 fusion.5
  9.4 8.8 %psum.7 = f32[512,1]{0,1:T(1,128)S(1)} all-reduce(f32[512,1]{0,1:T(1,128)S(1)} %bitcast.27), channel_id=1, replica_groups=mesh['my'=4,'mx'=4] {'mx'}, use_global_device_ids=true, to_apply=%region_1.0 | all-reduce | flops 512 | bytes 4096 | tf_op jit(solution)/shard_map/psum | solution.py:336
  18.2 1.7 convolution_convert_fusion.1
  19.9 0.5 convolution_convert_fusion.2
  20.4 1.3 convolution_convert_fusion
  21.8 1.1 pad_maximum_fusion
  23.0 0.6 reshape.242.gain
  23.6 0.1 iota_compare_fusion.1
  23.7 0.3 multiply_cosine_fusion.1
  24.1 20.9 %reduce-scatter.2.cloned.1.call-done = bf16[128,1152]{1,0:T(8,128)(2,1)} async-done(((bf16[512,1152]{1,0:T(8,128)(2,1)}), bf16[128,1152]{1,0:T(8,128)(2,1)}) %reduce-scatter.2.cloned.1.call-update) | async-done | bytes 294928 | tf_op jit(solution)/shard_map/reduce_scatter | solution.py:345
  44.9 1.0 convert_element_type.62
  46.0 0.3 fusion.35
  46.3 0.2 copy.23
  46.6 0.2 copy.31
  46.8 0.2 copy.30
  47.3 23.3 %broadcast_select_fusion.1 = (bf16[128,512,1,128]{3,1,2,0:T(8,128)(2,1)}, bf16[128,512,1,128]{3,1,2,0:T(8,128)(2,1)}) fusion(bf16[128,512,1,128]{3,1,2,0:T(8,128)(2,1)} %param.30, pred[128,512]{1,0:T(8,128)(4,1)S(1)} %get-tuple-element.16, bf16[128,128]{1,0:T(8,128)(2,1)S(1)} %pad_maximum_fusion.1, bf16[128,512,1,128]{3,1,2,0:T(8,128)(2,1)} %param.31, ...), kind=kLoop, calls=%fused_computation.5 | loop fusion | flops 16777216 | bytes 67239936 | tf_op jit(solution)/shard_map/jit(_where)/select_n | solution.py:355
  70.6 8.2 %fusion.4 = (f32[128,7]{1,0:T(8,128)S(1)}, f32[128,7,512]{2,1,0:T(8,128)S(1)}) fusion(pred[128,512]{1,0:T(8,128)(4,1)S(1)} %get-tuple-element.15, bf16[128,512,1,128]{3,1,2,0:T(8,128)(2,1)} %get-tuple-element.23, bf16[128,7,64]{2,1,0:T(8,128)(2,1)S(1)} %get-tuple-element.4, bf16[128,7,64]{2,1,0:T(8,128)(2,1)S(1)} %get-tuple-element.3), kind=kOutput, calls=%fused_computation.10 | convolution fusion | flops 119274624 | bytes 18910720 | tf_op jit(solution)/shard_map/bkgd,bskd->bkgs/dot_general | solution.py:317
  78.8 0.8 fusion.8
  79.6 7.3 %fusion.13 = bf16[128,7,128]{2,1,0:T(8,128)(2,1)S(1)} fusion(bf16[128,512,1,128]{3,1,2,0:T(8,128)(2,1)} %get-tuple-element.24, f32[128,7,512]{2,1,0:T(8,128)S(1)} %get-tuple-element.18, f32[128,7]{1,0:T(8,128)S(1)} %get-tuple-element.17, pred[128,512]{1,0:T(8,128)(4,1)S(1)} %get-tuple-element.15, f32[128,7]{1,0:T(8,128)S(1)} %fusion.8), kind=kOutput, calls=%fused_computation.18 | convolution fusion | flops 119504896 | bytes 18914304 | tf_op jit(solution)/shard_map/bkgs,bskd->bkgd/dot_general | solution.py:322
  86.9 0.2 copy.26
  87.1 0.8 copy.27.attn
  87.9 131.6 %attn_out_mlp.1 = bf16[512,896]{1,0:T(8,128)(2,1)} custom-call(bf16[128,896]{1,0:T(8,128)(2,1)} %copy.27.attn, bf16[512,896]{1,0:T(8,128)(2,1)} %x_in.1, bf16[1,896]{1,0:T(2,128)(2,1)} %reshape.242.gain, bf16[896,896]{1,0:T(8,128)(2,1)} %w_o.1, bf16[896,4736]{1,0:T(8,128)(2,1)} %w_gate.1, bf16[896,4736]{1,0:T(8,128)(2,1)} %w_up.1, bf16[4736,896]{1,0:T(8,128)(2,1)} %w_down.1), custom_call_target="tpu_custom_call" | custom-call | tf_op jit(solution)/shard_map/attn_out_mlp/pallas_call | solution.py:272
  219.5 2.2 copy.33
  (29 shorter events, 0.4 us)
Async XLA Ops:
  7.2 12.7 %copy-start = (bf16[512,896]{1,0:T(8,128)(2,1)S(1)}, bf16[512,896]{1,0:T(8,128)(2,1)}, u32[]{:S(2)}) copy-start(bf16[512,896]{1,0:T(8,128)(2,1)} %x_in.1) | copy-start | bytes 2752516
  7.2 12.7 %copy-start.5 = (bf16[896,128]{1,0:T(8,128)(2,1)S(1)}, bf16[896,128]{1,0:T(8,128)(2,1)}, u32[]{:S(2)}) copy-start(bf16[896,128]{1,0:T(8,128)(2,1)} %param.22) | copy-start | bytes 688132
  7.2 37.8 %reduce-scatter.2.cloned.1.call-start = ((), (), s32[]{:S(2)}) async-start(), calls=%async_computation.1 | async-start | bytes 1474560 | tf_op jit(solution)/shard_map/reduce_scatter | solution.py:345
  9.4 11.0 %copy-start.4 = (bf16[896,896]{1,0:T(8,128)(2,1)S(1)}, bf16[896,896]{1,0:T(8,128)(2,1)}, u32[]{:S(2)}) copy-start(bf16[896,896]{1,0:T(8,128)(2,1)} %param.20) | copy-start | bytes 4816900
  21.7 1.2 copy-start.6
  21.7 1.2 copy-start.7
  21.7 1.2 copy-start.3
  21.7 1.2 copy-start.1
  21.7 1.2 copy-start.2
Sparse Core Ops, SparseCore 0:
  23.0 21.8 reduce-scatter.1

commit v2 on v1

--- a/solution.py
+++ b/solution.py
@@ -1,3 +1,5 @@
+import math
+
 import jax
 import jax.numpy as jnp
 from jax import lax
@@ -8,7 +10,9 @@
 HEAD = 128
 NORM_EPS = 1e-6
 ROPE_THETA = 1000000.0
+VMEM_BYTES = 67043328
 CHUNKS = 4
+PLAN = ((0, 0), (1, 0), (0, 1), (1, 1), (2, 0), (2, 1), (3, 0), (0, 2), (1, 2), (4, 0), (3, 1), (5, 0), (4, 1), (2, 2), (0, 3), (1, 3), (5, 1), (3, 2), (2, 3), (4, 2), (3, 3), (6, 0), (5, 2), (4, 3), (6, 1), (5, 3), (7, 0), (8, 0), (6, 2), (7, 1), (8, 1), (9, 0), (6, 3), (9, 1), (10, 0), (7, 2), (8, 2), (10, 1), (7, 3), (8, 3), (9, 2), (9, 3), (10, 2), (10, 3))
 MESH_IDS = pl.DeviceIdType.MESH
 
 
@@ -38,13 +42,14 @@
 
 
 def column_to_lanes(col):
-    rows = col.shape[0]
-    return jnp.transpose(jnp.broadcast_to(col, (rows, rows)))[:8]
+    wide = jnp.broadcast_to(col, (col.shape[0], 128))
+    if col.shape[0] < 128:
+        wide = jnp.concatenate([wide] * (128 // col.shape[0]), axis=0)
+    return jnp.transpose(wide)[:8]
 
 
 def lanes_to_column(lanes):
-    width = lanes.shape[1]
-    return jnp.transpose(jnp.broadcast_to(lanes[:1], (width, width)))
+    return jnp.transpose(jnp.broadcast_to(lanes[:1], (128, 128)))
 
 
 def enter(axis_peers):
@@ -54,8 +59,8 @@
     pl.semaphore_wait(barrier, len(axis_peers))
 
 
-def mlp_kernel(attn, x_in, gain, w_o, w_gate, w_up, w_down, out,
-               wo_v, wg_v, wu_v, wd_v, x_v, attn_all, o_part, o_recv, mid, stat_send, stat_recv, h2,
+def mlp_kernel(attn_hbm, x_in, gain_hbm, w_o, w_gate, w_up, w_down, out,
+               attn, gain, wo_v, wg_v, wu_v, wd_v, x_v, attn_all, o_part, o_recv, mid, stat_send, stat_recv, h2,
                part, pair_recv, cross_send, cross_recv, act, acc, d_part, d_recv, out_all,
                w_sem, s_gather, r_gather, s_red, r_red, s_bc, r_bc, s_stat, r_stat, s_pair, r_pair,
                s_cross, r_cross, s_act, r_act, s_red2, r_red2, s_bc2, r_bc2, out_sem):
@@ -69,6 +74,7 @@
     def remote(src, dst, send, recv, axis, peer):
         return pltpu.make_async_remote_copy(src_ref=src, dst_ref=dst, send_sem=send, recv_sem=recv, device_id={axis: peer}, device_id_type=MESH_IDS)
 
+    first_loads = [pltpu.make_async_copy(attn_hbm, attn, w_sem.at[5]), pltpu.make_async_copy(gain_hbm, gain, w_sem.at[6])]
     loads = [
         pltpu.make_async_copy(w_o, wo_v, w_sem.at[0]),
         pltpu.make_async_copy(x_in.at[pl.ds(pl.multiple_of(my * CHUNKS * rb, CHUNKS * rb), CHUNKS * rb)], x_v, w_sem.at[1]),
@@ -76,7 +82,7 @@
         pltpu.make_async_copy(w_up, wu_v, w_sem.at[3]),
         pltpu.make_async_copy(w_down, wd_v, w_sem.at[4]),
     ]
-    for load in loads:
+    for load in first_loads + loads:
         load.start()
     enter([("mx", sib), ("mx", across), ("mx", across_sib)] + [("my", p) for p in my_list])
 
@@ -156,12 +162,12 @@
             loads[2].wait()
             loads[3].wait()
         total = stat_send[k] + stat_recv[k, 0] + stat_recv[k, 1] + stat_recv[k, 2]
-        scale = lanes_to_column(lax.rsqrt(total / (4 * hid) + NORM_EPS))
-        gain_row = gain[...].astype(jnp.float32)
+        scale = lanes_to_column(lax.rsqrt(total / (4 * hid) + NORM_EPS))[:rows]
+        gain_rows = gain[...].astype(jnp.float32)
         for t in range(hid // 128):
             cols = slice(t * 128, (t + 1) * 128)
             piece = mid[k, :, :, cols].reshape(rows, 128).astype(jnp.float32)
-            h2[:, cols] = (piece * scale * gain_row[:, cols]).astype(jnp.bfloat16)
+            h2[:, cols] = (piece * scale * gain_rows[t:t + 1]).astype(jnp.bfloat16)
 
         def body(off, tile):
             lhs = h2[...]
@@ -240,15 +246,13 @@
         for copy in out_copies(k):
             copy.start()
 
+    for load in first_loads:
+        load.wait()
     for k in range(CHUNKS):
         start_gather(k)
-    plan = [(forward_gather, 0), (out_proj, 0), (forward_gather, 1), (out_proj, 1), (own_block, 0), (own_block, 1), (stats, 0),
-            (forward_gather, 2), (out_proj, 2), (gate_up, 0), (stats, 1), (pair_sum, 0), (gate_up, 1), (own_block, 2), (forward_gather, 3), (out_proj, 3),
-            (pair_sum, 1), (stats, 2), (own_block, 3), (gate_up, 2), (stats, 3), (activate, 0), (pair_sum, 2), (gate_up, 3), (activate, 1), (pair_sum, 3),
-            (forward_act, 0), (down, 0), (activate, 2), (forward_act, 1), (down, 1), (out_block, 0), (activate, 3), (out_block, 1), (write_out, 0),
-            (forward_act, 2), (down, 2), (write_out, 1), (forward_act, 3), (down, 3), (out_block, 2), (out_block, 3), (write_out, 2), (write_out, 3)]
-    for stage, k in plan:
-        stage(k)
+    stages = (forward_gather, out_proj, own_block, stats, gate_up, pair_sum, activate, forward_act, down, out_block, write_out)
+    for stage, k in PLAN:
+        stages[stage](k)
 
     for k in range(CHUNKS):
         sends = list(gather_copies(k)) + reduce_copies(k, o_part, o_recv, s_red, r_red) + bcast_copies(k, mid, s_bc, r_bc) + stat_copies(k)
@@ -266,21 +270,21 @@
     rb = row_total // (4 * CHUNKS)
     bf16 = jnp.bfloat16
     f32 = jnp.float32
-    vmem = pl.BlockSpec(memory_space=pltpu.VMEM)
-    hbm = pl.BlockSpec(memory_space=pl.ANY)
+    hbm = pl.BlockSpec(memory_space=pltpu.HBM)
     dma = pltpu.SemaphoreType.DMA
     return pl.pallas_call(
         mlp_kernel,
         out_shape=jax.ShapeDtypeStruct((row_total, hid), bf16),
-        in_specs=[vmem, hbm, vmem, hbm, hbm, hbm, hbm],
+        in_specs=[hbm] * 7,
         out_specs=hbm,
         scratch_shapes=[
+            pltpu.VMEM(attn.shape, bf16), pltpu.VMEM((hid // 128, 128), bf16),
             pltpu.VMEM(w_o.shape, bf16), pltpu.VMEM(w_gate.shape, bf16), pltpu.VMEM(w_up.shape, bf16), pltpu.VMEM(w_down.shape, bf16),
             pltpu.VMEM((CHUNKS * rb, hid), bf16),
             pltpu.VMEM((CHUNKS, 4, rb, hid), bf16),
             pltpu.VMEM((CHUNKS, 4, rb, hid), bf16), pltpu.VMEM((CHUNKS, 3, rb, hid), bf16),
             pltpu.VMEM((CHUNKS, 4, rb, hid), bf16),
-            pltpu.VMEM((CHUNKS, 8, 4 * rb), f32), pltpu.VMEM((CHUNKS, 3, 8, 4 * rb), f32),
+            pltpu.VMEM((CHUNKS, 8, 128), f32), pltpu.VMEM((CHUNKS, 3, 8, 128), f32),
             pltpu.VMEM((4 * rb, hid), bf16),
             pltpu.VMEM((CHUNKS, 4, rb, 2 * ff), bf16), pltpu.VMEM((CHUNKS, 2, rb, 2 * ff), bf16),
             pltpu.VMEM((CHUNKS, rb, 2 * ff), bf16), pltpu.VMEM((CHUNKS, rb, 2 * ff), bf16),
@@ -288,74 +292,243 @@
             pltpu.VMEM((4 * rb, hid), f32),
             pltpu.VMEM((CHUNKS, 4, rb, hid), bf16), pltpu.VMEM((CHUNKS, 3, rb, hid), bf16),
             pltpu.VMEM((CHUNKS, 4, rb, hid), bf16),
-            dma((5,)),
+            dma((7,)),
             dma((CHUNKS, 3)), dma((CHUNKS, 3)), dma((CHUNKS, 3)), dma((CHUNKS, 3)), dma((CHUNKS, 3)), dma((CHUNKS, 3)),
             dma((CHUNKS, 3)), dma((CHUNKS, 3)), dma((CHUNKS, 2)), dma((CHUNKS, 2)),
             dma((CHUNKS,)), dma((CHUNKS,)), dma((CHUNKS, 3)), dma((CHUNKS, 3)),
             dma((CHUNKS, 3)), dma((CHUNKS, 3)), dma((CHUNKS, 3)), dma((CHUNKS, 3)), dma((CHUNKS, 4)),
         ],
-        compiler_params=pltpu.CompilerParams(collective_id=1, has_side_effects=True, vmem_limit_bytes=67043328),
+        compiler_params=pltpu.CompilerParams(collective_id=1, has_side_effects=True, vmem_limit_bytes=VMEM_BYTES),
         name="attn_out_mlp",
-    )(attn, x_in, gain.reshape(1, hid), w_o, w_gate, w_up, w_down)
-
-
-def apply_rotary(vectors, positions):
-    half_dim = HEAD // 2
-    inv_freq = ROPE_THETA ** (-2.0 * jnp.arange(half_dim, dtype=jnp.float32) / HEAD)
-    angles = positions.astype(jnp.float32)[:, None, None] * inv_freq
+    )(attn, x_in, gain.reshape(-1, 128), w_o, w_gate, w_up, w_down)
+
+
+def qkv_kernel(x_hbm, seq_hbm, gain_hbm, w_q_hbm, w_k_hbm, w_v_hbm, b_q_hbm, b_k_hbm, b_v_hbm, q_out, k_out, v_out,
+               x, seq, gain, w_q, w_k, w_v, b_q, b_k, b_v, load_sem, stat_send, stat_recv, h1, part, pair_recv, cross_send, cross_recv,
+               s_stat, r_stat, s_pair, r_pair, s_cross, r_cross):
+    mx, sib, across, across_sib = mx_peers()
+    rows, hid = x.shape
+    block = rows // 4
+    q_cols = w_q.shape[1]
+    loads = [pltpu.make_async_copy(src, dst, load_sem.at[i]) for i, (src, dst) in enumerate((
+        (x_hbm, x), (gain_hbm, gain), (w_q_hbm, w_q), (w_k_hbm, w_k), (w_v_hbm, w_v), (b_q_hbm, b_q), (b_k_hbm, b_k), (b_v_hbm, b_v), (seq_hbm, seq)))]
+    for load in loads:
+        load.start()
+    enter([("mx", sib), ("mx", across), ("mx", across_sib)])
+    loads[0].wait()
+
+    def remote(src, dst, send, recv, peer):
+        return pltpu.make_async_remote_copy(src_ref=src, dst_ref=dst, send_sem=send, recv_sem=recv, device_id={"mx": peer}, device_id_type=MESH_IDS)
+
+    for j in range(4):
+        piece = x[j * block:(j + 1) * block].astype(jnp.float32)
+        stat_send[:, j * block:(j + 1) * block] = column_to_lanes(jnp.sum(piece * piece, axis=1, keepdims=True))
+    stat_copies = [remote(stat_send, stat_recv.at[d], s_stat.at[d], r_stat.at[d], p) for d, p in enumerate((sib, across, across_sib))]
+    for copy in stat_copies:
+        copy.start()
+    for load in loads[1:]:
+        load.wait()
+    for copy in stat_copies:
+        copy.wait_recv()
+    total = stat_send[...] + stat_recv[0] + stat_recv[1] + stat_recv[2]
+    stat_recv[0] = lax.rsqrt(total / (4 * hid) + NORM_EPS)
+    gain_rows = gain[...].astype(jnp.float32)
+    pair_copies = [remote(part.at[across_sib], pair_recv.at[0], s_pair.at[0], r_pair.at[0], sib),
+                   remote(part.at[sib], pair_recv.at[1], s_pair.at[1], r_pair.at[1], sib)]
+    cross = remote(cross_send, cross_recv, s_cross, r_cross, across)
+
+    def project(j):
+        start = pl.multiple_of(j * block, block)
+        scale = lanes_to_column(stat_recv[0, :, pl.ds(start, block)])
+        for t in range(hid // 128):
+            cols = slice(t * 128, (t + 1) * 128)
+            h1[:, cols] = (x[pl.ds(start, block), cols].astype(jnp.float32) * scale * gain_rows[t:t + 1]).astype(jnp.bfloat16)
+        lhs = h1[...]
+        off = 0
+        for w in (w_q, w_k, w_v):
+            part[j, :, off:off + w.shape[1]] = jnp.dot(lhs, w[...], preferred_element_type=jnp.float32).astype(jnp.bfloat16)
+            off += w.shape[1]
+
+    project(across_sib)
+    pair_copies[0].start()
+    project(across)
+    pair_copies[0].wait_recv()
+    cross_send[...] = (part[across].astype(jnp.float32) + pair_recv[0].astype(jnp.float32)).astype(jnp.bfloat16)
+    cross.start()
+    project(sib)
+    pair_copies[1].start()
+    project(mx)
+    lane = lax.broadcasted_iota(jnp.int32, (block, HEAD), 1)
+    inv_freq = jnp.exp(lax.rem(lane, HEAD // 2).astype(jnp.float32) * (-2.0 / HEAD * math.log(ROPE_THETA)))
+    angles = lanes_to_column(seq[...].astype(jnp.float32)) * inv_freq
     cos_tab = jnp.cos(angles)
-    sin_tab = jnp.sin(angles)
-    lower_half = vectors[..., :half_dim]
-    upper_half = vectors[..., half_dim:]
-    return jnp.concatenate([lower_half * cos_tab - upper_half * sin_tab, upper_half * cos_tab + lower_half * sin_tab], axis=-1)
-
-
-def attend_local(q_rot, k_cache_out, v_cache_out, seq_lens):
-    row_count, seq_len, kv_heads, _ = k_cache_out.shape
-    q_heads = q_rot.shape[1]
-    q_grouped = q_rot.reshape(row_count, kv_heads, q_heads // kv_heads, HEAD)
-    scores = jnp.einsum("bkgd,bskd->bkgs", q_grouped, k_cache_out, preferred_element_type=jnp.float32) * HEAD ** -0.5
-    visible = (jnp.arange(seq_len)[None, :] <= seq_lens[:, None])[:, None, None, :]
-    scores = jnp.where(visible, scores, -jnp.inf)
-    weights = jnp.exp(scores - jnp.max(scores, axis=-1, keepdims=True))
-    weight_sum = jnp.sum(weights, axis=-1, keepdims=True)
-    weighted = jnp.einsum("bkgs,bskd->bkgd", weights.astype(jnp.bfloat16), v_cache_out, preferred_element_type=jnp.float32)
-    return (weighted / weight_sum).astype(jnp.bfloat16).reshape(row_count, q_heads * HEAD)
+    sin_tab = jnp.where(lane < HEAD // 2, -jnp.sin(angles), jnp.sin(angles))
+    pair_copies[1].wait_recv()
+    cross.wait_recv()
+
+    def total_of(off, bias):
+        cols = slice(off, off + HEAD)
+        return part[mx, :, cols].astype(jnp.float32) + pair_recv[1, :, cols].astype(jnp.float32) + cross_recv[:, cols].astype(jnp.float32) + bias.astype(jnp.float32)
+
+    def rotated(vals):
+        return (vals * cos_tab + pltpu.roll(vals, HEAD // 2, 1) * sin_tab).astype(jnp.bfloat16).astype(jnp.float32)
+
+    heads = q_cols // HEAD
+    for h in range(heads):
+        q_out[:, h, :] = rotated(total_of(h * HEAD, b_q[h:h + 1]))
+    for h in range(heads, q_out.shape[1]):
+        q_out[:, h, :] = jnp.zeros((block, HEAD), jnp.float32)
+    k_out[...] = rotated(total_of(q_cols, b_k[...]))
+    v_out[...] = total_of(q_cols + HEAD, b_v[...]).astype(jnp.bfloat16).astype(jnp.float32)
+    for copy in stat_copies + pair_copies + [cross]:
+        copy.wait_send()
+
+
+def qkv_call(x_in, seq_lens, gain, w_q, w_k, w_v, b_q, b_k, b_v):
+    rows, hid = x_in.shape
+    block = rows // 4
+    cols = w_q.shape[1] + w_k.shape[1] + w_v.shape[1]
+    heads_pad = -(-w_q.shape[1] // HEAD // 8) * 8
+    bf16 = jnp.bfloat16
+    f32 = jnp.float32
+    vmem = pl.BlockSpec(memory_space=pltpu.VMEM)
+    hbm = pl.BlockSpec(memory_space=pltpu.HBM)
+    dma = pltpu.SemaphoreType.DMA
+    return pl.pallas_call(
+        qkv_kernel,
+        out_shape=(jax.ShapeDtypeStruct((block, heads_pad, HEAD), f32), jax.ShapeDtypeStruct((block, HEAD), f32), jax.ShapeDtypeStruct((block, HEAD), f32)),
+        in_specs=[hbm] * 9,
+        out_specs=(vmem, vmem, vmem),
+        scratch_shapes=[
+            pltpu.VMEM(x_in.shape, bf16), pltpu.VMEM((1, block), jnp.int32), pltpu.VMEM((hid // 128, 128), bf16),
+            pltpu.VMEM(w_q.shape, bf16), pltpu.VMEM(w_k.shape, bf16), pltpu.VMEM(w_v.shape, bf16),
+            pltpu.VMEM((w_q.shape[1] // HEAD, HEAD), bf16), pltpu.VMEM((1, HEAD), bf16), pltpu.VMEM((1, HEAD), bf16), dma((9,)),
+            pltpu.VMEM((8, rows), f32), pltpu.VMEM((3, 8, rows), f32), pltpu.VMEM((block, hid), bf16),
+            pltpu.VMEM((4, block, cols), bf16), pltpu.VMEM((2, block, cols), bf16), pltpu.VMEM((block, cols), bf16), pltpu.VMEM((block, cols), bf16),
+            dma((3,)), dma((3,)), dma((2,)), dma((2,)), dma, dma,
+        ],
+        compiler_params=pltpu.CompilerParams(collective_id=0, has_side_effects=True, vmem_limit_bytes=VMEM_BYTES),
+        name="norm_qkv",
+    )(x_in, seq_lens.reshape(1, block), gain.reshape(-1, 128), w_q, w_k, w_v, b_q.reshape(-1, HEAD), b_k.reshape(1, -1), b_v.reshape(1, -1))
+
+
+GROUP_ROWS = 4
+SLOTS = 8
+AHEAD = 4
+
+
+def attend_kernel(seq_hbm, q_hbm, k_new_hbm, v_new_hbm, k_cache, v_cache, attn_hbm, k_out, v_out, k_buf, v_buf, heads_out, attn, seq, q, k_new, v_new, in_sem, out_sem, misc_sem):
+    batch, length, _ = k_cache.shape
+    groups = batch // GROUP_ROWS
+
+    def fetch(i):
+        slot = lax.rem(i, SLOTS)
+        rows = pl.ds(i * GROUP_ROWS, GROUP_ROWS)
+        return (pltpu.make_async_copy(k_cache.at[rows], k_buf.at[slot], in_sem.at[0, slot]),
+                pltpu.make_async_copy(v_cache.at[rows], v_buf.at[slot], in_sem.at[1, slot]))
+
+    def flush(i):
+        slot = lax.rem(i, SLOTS)
+        rows = pl.ds(i * GROUP_ROWS, GROUP_ROWS)
+        return (pltpu.make_async_copy(k_buf.at[slot], k_out.at[rows], out_sem.at[0, slot]),
+                pltpu.make_async_copy(v_buf.at[slot], v_out.at[rows], out_sem.at[1, slot]))
+
+    loads = [pltpu.make_async_copy(src, dst, misc_sem.at[i]) for i, (src, dst) in enumerate(((seq_hbm, seq), (q_hbm, q), (k_new_hbm, k_new), (v_new_hbm, v_new)))]
+    for load in loads:
+        load.start()
+    for i in range(AHEAD):
+        for copy in fetch(jnp.int32(i)):
+            copy.start()
+    for load in loads:
+        load.wait()
+
+
+    def step(i, carry):
+        slot = lax.rem(i, SLOTS)
+        for copy in fetch(i):
+            copy.wait()
+        tile_row = lax.broadcasted_iota(jnp.int32, (16, HEAD), 0)
+        for r in range(GROUP_ROWS):
+            b = i * GROUP_ROWS + r
+            pos = seq[b]
+            base = pl.multiple_of(pos // 16 * 16, 16)
+            hit = tile_row == pos - base
+            for buf, new in ((k_buf, k_new), (v_buf, v_new)):
+                tile = buf[slot, r, pl.ds(base, 16), :].astype(jnp.float32)
+                buf[slot, r, pl.ds(base, 16), :] = jnp.where(hit, new[pl.ds(b, 1), :], tile).astype(jnp.bfloat16)
+        scores = []
+        for r in range(GROUP_ROWS):
+            b = i * GROUP_ROWS + r
+            s = lax.dot_general(q[b].astype(jnp.bfloat16), k_buf[slot, r], (((1,), (1,)), ((), ())), preferred_element_type=jnp.float32) * HEAD ** -0.5
+            t = lax.broadcasted_iota(jnp.int32, s.shape, 1)
+            scores.append(jnp.where(t <= seq[b], s, -jnp.inf))
+        for r in range(GROUP_ROWS):
+            b = i * GROUP_ROWS + r
+            s = scores[r]
+            w = jnp.exp(s - jnp.max(s, axis=1, keepdims=True))
+            total = jnp.sum(w, axis=1, keepdims=True)
+            o = jnp.dot(w.astype(jnp.bfloat16), v_buf[slot, r], preferred_element_type=jnp.float32)
+            heads_out[b] = o / total
+        for copy in flush(i):
+            copy.start()
+
+        @pl.when(i + AHEAD < groups)
+        def _():
+            @pl.when(i + AHEAD >= SLOTS)
+            def _():
+                for copy in flush(i + AHEAD - SLOTS):
+                    copy.wait()
+
+            for copy in fetch(i + AHEAD):
+                copy.start()
+
+        return carry
+
+    lax.fori_loop(0, groups, step, 0)
+    for h in range(attn.shape[1] // HEAD):
+        attn[:, h * HEAD:(h + 1) * HEAD] = heads_out[:, h, :].astype(jnp.bfloat16)
+    attn_store = pltpu.make_async_copy(attn, attn_hbm, misc_sem.at[4])
+    attn_store.start()
+    for i in range(groups - SLOTS, groups):
+        for copy in flush(jnp.int32(i)):
+            copy.wait()
+    attn_store.wait()
+
+
+def attend_call(seq_lens, q, k_new, v_new, k_cache, v_cache, q_cols):
+    batch, length, _, _ = k_cache.shape
+    bf16 = jnp.bfloat16
+    f32 = jnp.float32
+    hbm = pl.BlockSpec(memory_space=pltpu.HBM)
+    dma = pltpu.SemaphoreType.DMA
+    flat = (batch, length, HEAD)
+    attn, k_out, v_out = pl.pallas_call(
+        attend_kernel,
+        out_shape=(jax.ShapeDtypeStruct((batch, q_cols), bf16), jax.ShapeDtypeStruct(flat, bf16), jax.ShapeDtypeStruct(flat, bf16)),
+        in_specs=[hbm] * 6,
+        out_specs=(hbm, hbm, hbm),
+        scratch_shapes=[
+            pltpu.VMEM((SLOTS, GROUP_ROWS, length, HEAD), bf16), pltpu.VMEM((SLOTS, GROUP_ROWS, length, HEAD), bf16),
+            pltpu.VMEM(q.shape, f32), pltpu.VMEM((batch, q_cols), bf16), pltpu.SMEM((batch,), jnp.int32),
+            pltpu.VMEM(q.shape, f32), pltpu.VMEM(k_new.shape, f32), pltpu.VMEM(v_new.shape, f32),
+            dma((2, SLOTS)), dma((2, SLOTS)), dma((5,)),
+        ],
+        compiler_params=pltpu.CompilerParams(vmem_limit_bytes=VMEM_BYTES),
+        name="attend_and_update",
+    )(seq_lens, q, k_new, v_new, k_cache.reshape(flat), v_cache.reshape(flat))
+    return attn, k_out.reshape(k_cache.shape), v_out.reshape(v_cache.shape)
 
 
 def solution(mesh):
-    mx_size = mesh.shape["mx"]
     act_spec = P(None, "mx")
     cache_spec = P("mx", None, "my", None)
     in_specs = (act_spec, P("mx"), P("mx"), P("mx"), P("mx", "my"), P("my"), P("mx", "my"), P("my"), P("mx", "my"), P("my"), P("my", "mx"), P("mx", "my"), P("mx", "my"), P("my", "mx"), cache_spec, cache_spec)
     out_specs = (act_spec, cache_spec, cache_spec)
 
     def local_layer(x_in, seq_lens, gain_attn, gain_mlp, w_q, b_q, w_k, b_k, w_v, b_v, w_o, w_gate, w_up, w_down, k_cache, v_cache):
-        hidden = x_in.shape[1] * mx_size
-        x_f32 = x_in.astype(jnp.float32)
-        attn_sq = lax.psum(jnp.sum(x_f32 * x_f32, axis=1, keepdims=True), "mx")
-        normed = (x_f32 * lax.rsqrt(attn_sq / hidden + NORM_EPS) * gain_attn.astype(jnp.float32)).astype(jnp.bfloat16)
-        q_cols = w_q.shape[1]
-        kv_cols = w_k.shape[1]
-        partials = jnp.concatenate([
-            jnp.dot(normed, w_q, preferred_element_type=jnp.float32).astype(jnp.bfloat16),
-            jnp.dot(normed, w_k, preferred_element_type=jnp.float32).astype(jnp.bfloat16),
-            jnp.dot(normed, w_v, preferred_element_type=jnp.float32).astype(jnp.bfloat16),
-        ], axis=1)
-        projected = lax.psum_scatter(partials, "mx", scatter_dimension=0, tiled=True).astype(jnp.float32)
-        row_count = projected.shape[0]
-        kv_heads = kv_cols // HEAD
-        q_vals = projected[:, :q_cols] + b_q.astype(jnp.float32)
-        k_vals = projected[:, q_cols:q_cols + kv_cols] + b_k.astype(jnp.float32)
-        v_vals = projected[:, q_cols + kv_cols:] + b_v.astype(jnp.float32)
-        q_rot = apply_rotary(q_vals.reshape(row_count, q_cols // HEAD, HEAD), seq_lens).astype(jnp.bfloat16)
-        k_rot = apply_rotary(k_vals.reshape(row_count, kv_heads, HEAD), seq_lens).astype(jnp.bfloat16)
-        v_new = v_vals.reshape(row_count, kv_heads, HEAD).astype(jnp.bfloat16)
-        at_slot = (jnp.arange(k_cache.shape[1])[None, :] == seq_lens[:, None])[:, :, None, None]
-        k_cache_out = jnp.where(at_slot, k_rot[:, None], k_cache)
-        v_cache_out = jnp.where(at_slot, v_new[:, None], v_cache)
-        attn_rows = attend_local(q_rot, k_cache_out, v_cache_out, seq_lens)
-        x_out = mlp_call(attn_rows, x_in, gain_mlp, w_o, w_gate, w_up, w_down)
+        q, k_new, v_new = qkv_call(x_in, seq_lens, gain_attn, w_q, w_k, w_v, b_q, b_k, b_v)
+        attn, k_cache_out, v_cache_out = attend_call(seq_lens, q, k_new, v_new, k_cache, v_cache, w_q.shape[1])
+        x_out = mlp_call(attn, x_in, gain_mlp, w_o, w_gate, w_up, w_down)
         return x_out, k_cache_out, v_cache_out
 
     return jax.shard_map(local_layer, mesh=mesh, in_specs=in_specs, out_specs=out_specs, check_vma=False)

time: 229 us -> 177 us (0.77)
  Pallas kernels: 132 us -> 174 us
  other arithmetic: 29.5 us -> 0 us
  waiting for transfers between devices: 20.9 us -> 0 us
  matrix products: 18.9 us -> 0 us
  between operations: 14.3 us -> 0.66 us
  blocking collectives: 8.77 us -> 0 us
  local copies, waits for them, and re-layouts: 4.58 us -> 2.18 us
    pallas_call x0 -> x2, Pallas kernels: none -> 42.9 us  [the longest x1 24.5 us: attend_call(): pl.pallas_call(attend_kernel, out_shape=(jax.ShapeDtypeStruct((batch, q_c...]
    select_n x1 -> x0, other arithmetic: 23.3 us -> none  [local_layer(): k_cache_out = jnp.where(at_slot, k_rot[:, None], k_cache)]
    reduce_scatter x1 -> x0, waiting for transfers between devices: 20.9 us -> none  [local_layer(): lax.psum_scatter(partials, 'mx', scatter_dimension=0, tiled=True)]
    dot_general x5 -> x0, matrix products: 18.9 us -> none  [the longest x1 8.17 us: attend_local(): jnp.einsum('bkgd,bskd->bkgs', q_grouped, k_cache_out, preferred_element_t...]
    psum x1 -> x0, blocking collectives: 8.77 us -> none  [local_layer(): attn_sq = lax.psum(jnp.sum(x_f32 * x_f32, axis=1, keepdims=True), 'mx')]
  transfers between devices with their start and end apart: 1 -> 0, of which waited for: 1 -> 0; matrix products, arithmetic and copies ran while one was open for 0% -> 0% of each run, Pallas kernels for 0% -> 0%
where the time goes in v2:
time: 177 us
  Pallas kernels  174 us (98%)
  local copies, waits for them, and re-layouts  2.18 us (1%)
    pallas_call x1, Pallas kernels, mlp_call(): pl.pallas_call(mlp_kernel, out_shape=jax.ShapeDtypeStruct((row_total, hid...  131 us
    pallas_call x1, Pallas kernels, attend_call(): pl.pallas_call(attend_kernel, out_shape=(jax.ShapeDtypeStruct((batch, q_c...  24.5 us
    pallas_call x1, Pallas kernels, qkv_call(): pl.pallas_call(qkv_kernel, out_shape=(jax.ShapeDtypeStruct((block, heads_...  18.3 us

profile of v2, /device:TPU:0, one launch (start us, length us, event | category | flops | bytes accessed | tf_op | source)
XLA Modules:
  0.0 176.5 jit_solution(10716405232257886807)
XLA Ops:
  0.6 18.3 %norm_qkv.1 = (f32[128,8,128]{2,1,0:T(8,128)}, f32[128,128]{1,0:T(8,128)}, f32[128,128]{1,0:T(8,128)}) custom-call(bf16[512,896]{1,0:T(8,128)(2,1)} %x_in.1, s32[1,128]{1,0:T(1,128)} %bitcast.19, bf16[7,128]{1,0:T(8,128)(2,1)} %bitcast.16, bf16[896,896]{1,0:T(8,128)(2,1)} %w_q_hbm.1, bf16[896,128]{1,0:T(8,128)(2,1)} %w_k_hbm.1, bf16[896,128]{1,0:T(8,128)(2,1)} %w_v_hbm.1, ...), custom_call_target="tpu_custom_call" | custom-call | tf_op jit(solution)/shard_map/norm_qkv/pallas_call | solution.py:397
  19.0 24.5 %attend_and_update.1 = (bf16[128,896]{1,0:T(8,128)(2,1)}, bf16[128,512,128]{2,1,0:T(8,128)(2,1)}, bf16[128,512,128]{2,1,0:T(8,128)(2,1)}) custom-call(s32[128]{0:T(128)} %seq_hbm.1, f32[128,8,128]{2,1,0:T(8,128)} %get-tuple-element.9.q_hbm, f32[128,128]{1,0:T(8,128)} %get-tuple-element.10.k_new_hbm, f32[128,128]{1,0:T(8,128)} %get-tuple-element.11.v_new_hbm, ...), custom_call_target="tpu_custom_call" | custom-call | tf_op jit(solution)/shard_map/attend_and_update/pallas_call | solution.py:505
  43.5 130.8 %attn_out_mlp.1 = bf16[512,896]{1,0:T(8,128)(2,1)} custom-call(bf16[128,896]{1,0:T(8,128)(2,1)} %get-tuple-element.12.attn_hbm, bf16[512,896]{1,0:T(8,128)(2,1)} %x_in.1, bf16[7,128]{1,0:T(8,128)(2,1)} %bitcast.18, bf16[896,896]{1,0:T(8,128)(2,1)} %w_o.1, bf16[896,4736]{1,0:T(8,128)(2,1)} %w_gate.1, bf16[896,4736]{1,0:T(8,128)(2,1)} %w_up.1, ...), custom_call_target="tpu_custom_call" | custom-call | tf_op jit(solution)/shard_map/attn_out_mlp/pallas_call | solution.py:275
  174.3 2.2 %copy.22 = bf16[512,896]{1,0:T(8,128)(2,1)} copy(bf16[512,896]{1,0:T(8,128)(2,1)} %attn_out_mlp.1) | data formatting | bytes 1835008

commit v3 on v2

v3 whole, which is shorter than its diff:
```python
import math

import jax
import jax.numpy as jnp
from jax import lax
from jax.experimental import pallas as pl
from jax.experimental.pallas import tpu as pltpu
from jax.sharding import PartitionSpec as P

HEAD = 128
NORM_EPS = 1e-6
ROPE_THETA = 1000000.0
VMEM_BYTES = 67043328
MLP_VMEM_BYTES = 65900000
CHUNK_ROWS = (16, 32, 32, 32, 16)
CHUNK_STARTS = (0, 16, 48, 80, 112)
SPAN_TILES = (12, 12, 13)
PLAN = ((0, 0, 0), (1, 0, 0), (0, 1, 0), (0, 2, 0), (1, 1, 0), (0, 3, 0), (0, 4, 0), (2, 0, 0), (1, 2, 0), (1, 3, 0), (1, 4, 0), (2, 1, 0), (3, 0, 0), (2, 2, 0), (4, 0, 0), (4, 0, 1), (5, 0, 0), (4, 0, 2), (5, 0, 1), (3, 1, 0), (5, 0, 2), (2, 3, 0), (6, 0, 0), (4, 1, 0), (6, 0, 1), (4, 1, 1), (5, 1, 0), (7, 0, 0), (7, 0, 1), (5, 1, 1), (6, 0, 2), (8, 0, 0), (8, 0, 1), (4, 1, 2), (6, 1, 0), (3, 2, 0), (5, 1, 2), (3, 3, 0), (4, 2, 0), (7, 0, 2), (5, 2, 0), (8, 0, 2), (7, 1, 0), (6, 1, 1), (8, 1, 0), (4, 2, 1), (6, 1, 2), (5, 2, 1), (4, 2, 2), (6, 2, 0), (5, 2, 2), (9, 0, 0), (4, 3, 0), (7, 1, 1), (4, 3, 1), (7, 1, 2), (8, 1, 1), (5, 3, 0), (8, 1, 2), (5, 3, 1), (4, 3, 2), (6, 2, 1), (2, 4, 0), (5, 3, 2), (7, 2, 0), (10, 0, 0), (8, 2, 0), (3, 4, 0), (9, 1, 0), (6, 2, 2), (4, 4, 0), (4, 4, 1), (5, 4, 0), (6, 3, 0), (5, 4, 1), (4, 4, 2), (10, 1, 0), (5, 4, 2), (6, 3, 1), (7, 2, 1), (8, 2, 1), (6, 3, 2), (7, 2, 2), (8, 2, 2), (6, 4, 0), (7, 3, 0), (8, 3, 0), (6, 4, 1), (9, 2, 0), (6, 4, 2), (7, 3, 1), (8, 3, 1), (7, 3, 2), (7, 4, 0), (7, 4, 1), (8, 3, 2), (7, 4, 2), (8, 4, 0), (8, 4, 1), (8, 4, 2), (10, 2, 0), (9, 3, 0), (9, 4, 0), (10, 3, 0), (10, 4, 0))
MESH_IDS = pl.DeviceIdType.MESH


def in_hbm(array):
    return pltpu.with_memory_space_constraint(array, pltpu.HBM)


def in_vmem(array):
    return pltpu.with_memory_space_constraint(array, pltpu.VMEM)


def over_tiles(total, tile, body):
    count = total // tile

    def step(i, carry):
        body(pl.multiple_of(i * tile, tile), tile)
        return carry

    lax.fori_loop(0, count, step, 0)
    if total % tile:
        body(count * tile, total % tile)


def mx_peers():
    me = lax.axis_index("mx")
    core = lax.rem(me, 2)
    sib = me + 1 - 2 * core
    return me, sib, lax.rem(me + 2, 4), lax.rem(sib + 2, 4)


def my_peers():
    me = lax.axis_index("my")
    flip = me + 1 - 2 * lax.rem(me, 2)
    return me, (flip, lax.rem(me + 2, 4), lax.rem(flip + 2, 4))


def column_to_lanes(col):
    wide = jnp.broadcast_to(col, (col.shape[0], 128))
    if col.shape[0] < 128:
        wide = jnp.concatenate([wide] * (128 // col.shape[0]), axis=0)
    return jnp.transpose(wide)[:8]


def lanes_to_column(lanes):
    return jnp.transpose(jnp.broadcast_to(lanes[:1], (128, 128)))


def enter(axis_peers):
    barrier = pltpu.get_barrier_semaphore()
    for axis, peer in axis_peers:
        pl.semaphore_signal(barrier, inc=1, device_id={axis: peer}, device_id_type=MESH_IDS)
    pl.semaphore_wait(barrier, len(axis_peers))


def mlp_kernel(attn_hbm, x_in, gain_hbm, w_o, w_gate, w_up, w_down, out,
               attn, gain, wo_v, wg_v, wu_v, wd_v, x_v, attn_all, o_part, o_recv, mid, stat_send, stat_recv, h2,
               part, pair_recv, cross_send, cross_recv, act, acc, d_part, d_recv,
               w_sem, s_gather, r_gather, s_red, r_red, s_bc, r_bc, s_stat, r_stat, s_pair, r_pair,
               s_cross, r_cross, s_act, r_act, s_red2, r_red2, s_bc2, r_bc2):
    mx, sib, across, across_sib = mx_peers()
    my, my_list = my_peers()
    block = attn.shape[0]
    hid = mid.shape[2]
    ff = wg_v.shape[1]
    chunks = len(CHUNK_ROWS)
    spans = []
    for tiles in SPAN_TILES:
        start = spans[-1][1] if spans else 0
        spans.append((start, start + tiles * (ff // sum(SPAN_TILES))))

    def rows_of(k):
        return pl.ds(CHUNK_STARTS[k], CHUNK_ROWS[k])

    def pair_cols(h):
        return pl.ds(2 * spans[h][0], 2 * (spans[h][1] - spans[h][0]))

    def span_cols(h):
        return pl.ds(spans[h][0], spans[h][1] - spans[h][0])

    def remote(src, dst, send, recv, axis, peer):
        return pltpu.make_async_remote_copy(src_ref=src, dst_ref=dst, send_sem=send, recv_sem=recv, device_id={axis: peer}, device_id_type=MESH_IDS)

    first_loads = [pltpu.make_async_copy(attn_hbm, attn, w_sem.at[5]), pltpu.make_async_copy(gain_hbm, gain, w_sem.at[6])]
    loads = [
        pltpu.make_async_copy(w_o, wo_v, w_sem.at[0]),
        pltpu.make_async_copy(x_in.at[pl.ds(pl.multiple_of(my * block, block), block)], x_v, w_sem.at[1]),
        pltpu.make_async_copy(w_gate, wg_v, w_sem.at[2]),
        pltpu.make_async_copy(w_up, wu_v, w_sem.at[3]),
        pltpu.make_async_copy(w_down, wd_v, w_sem.at[4]),
    ]
    for load in first_loads + loads:
        load.start()
    enter([("mx", sib), ("mx", across), ("mx", across_sib)] + [("my", p) for p in my_list])

    def gather_to_across(k):
        return remote(attn.at[rows_of(k)], attn_all.at[mx, rows_of(k)], s_gather.at[k, 0], r_gather.at[k, 0], "mx", across)

    def gather_to_sib(k):
        return remote(attn.at[rows_of(k)], attn_all.at[mx, rows_of(k)], s_gather.at[k, 1], r_gather.at[k, 1], "mx", sib)

    def gather_forward(k):
        return remote(attn_all.at[across, rows_of(k)], attn_all.at[across, rows_of(k)], s_gather.at[k, 2], r_gather.at[k, 2], "mx", sib)

    def reduce_copies(k, src, dst, send, recv):
        return [remote(src.at[p, rows_of(k)], dst.at[d, rows_of(k)], send.at[k, d], recv.at[k, d], "my", p) for d, p in enumerate(my_list)]

    def bcast_copies(k, buf, send, recv):
        return [remote(buf.at[my, rows_of(k)], buf.at[my, rows_of(k)], send.at[k, d], recv.at[k, d], "my", p) for d, p in enumerate(my_list)]

    def out_bcast(k):
        rows = pl.ds(pl.multiple_of(my * block + CHUNK_STARTS[k], 16), CHUNK_ROWS[k])
        return [remote(out.at[rows], out.at[rows], s_bc2.at[k, d], r_bc2.at[k, d], "my", p) for d, p in enumerate(my_list)]

    def stat_copies(k):
        return [remote(stat_send.at[k], stat_recv.at[k, d], s_stat.at[k, d], r_stat.at[k, d], "mx", p) for d, p in enumerate((sib, across, across_sib))]

    def pair_first(k, h):
        return remote(part.at[across_sib, rows_of(k), pair_cols(h)], pair_recv.at[0, rows_of(k), pair_cols(h)], s_pair.at[k, 2 * h], r_pair.at[k, 2 * h], "mx", sib)

    def pair_second(k, h):
        return remote(part.at[sib, rows_of(k), pair_cols(h)], pair_recv.at[1, rows_of(k), pair_cols(h)], s_pair.at[k, 2 * h + 1], r_pair.at[k, 2 * h + 1], "mx", sib)

    def cross_copy(k, h):
        return remote(cross_send.at[rows_of(k), pair_cols(h)], cross_recv.at[rows_of(k), pair_cols(h)], s_cross.at[k, h], r_cross.at[k, h], "mx", across)

    def act_copy(k, h, which):
        owner, peer = ((mx, across), (mx, sib), (across, sib))[which]
        ref = act.at[owner, rows_of(k), span_cols(h)]
        return remote(ref, ref, s_act.at[k, 3 * h + which], r_act.at[k, 3 * h + which], "mx", peer)

    def forward_gather(k, h):
        gather_to_across(k).wait_recv()
        gather_forward(k).start()

    def out_proj(k, h):
        rb = CHUNK_ROWS[k]
        gather_to_sib(k).wait_recv()
        gather_forward(k).wait_recv()
        if k == 0:
            loads[0].wait()
        rows_in = attn_all[:, rows_of(k), :].reshape(4 * rb, hid)
        o_part[:, rows_of(k), :] = jnp.dot(rows_in, wo_v[...], preferred_element_type=jnp.float32).astype(jnp.bfloat16).reshape(4, rb, hid)
        for copy in reduce_copies(k, o_part, o_recv, s_red, r_red):
            copy.start()

    def own_block(k, h):
        for copy in reduce_copies(k, o_part, o_recv, s_red, r_red):
            copy.wait_recv()
        if k == 0:
            loads[1].wait()
        total = o_part[my, rows_of(k), :].astype(jnp.float32)
        for d in range(3):
            total += o_recv[d, rows_of(k), :].astype(jnp.float32)
        mid[my, rows_of(k), :] = (x_v[rows_of(k), :].astype(jnp.float32) + total).astype(jnp.bfloat16)
        for copy in bcast_copies(k, mid, s_bc, r_bc):
            copy.start()

    def stats(k, h):
        for copy in bcast_copies(k, mid, s_bc, r_bc):
            copy.wait_recv()
        rows_f32 = mid[:, rows_of(k), :].reshape(4 * CHUNK_ROWS[k], hid).astype(jnp.float32)
        stat_send[k] = column_to_lanes(jnp.sum(rows_f32 * rows_f32, axis=1, keepdims=True))
        for copy in stat_copies(k):
            copy.start()

    def gate_up(k, h):
        rb = CHUNK_ROWS[k]
        rows = 4 * rb
        if h == 0:
            for copy in stat_copies(k):
                copy.wait_recv()
            total = stat_send[k] + stat_recv[k, 0] + stat_recv[k, 1] + stat_recv[k, 2]
            scale = lanes_to_column(lax.rsqrt(total / (4 * hid) + NORM_EPS))[:rows]
            gain_rows = gain[...].astype(jnp.float32)
            for t in range(hid // 128):
                cols = slice(t * 128, (t + 1) * 128)
                piece = mid[:, rows_of(k), cols].reshape(rows, 128).astype(jnp.float32)
                h2[k % 2, :rows, cols] = (piece * scale * gain_rows[t:t + 1]).astype(jnp.bfloat16)
            if k == 0:
                loads[2].wait()
                loads[3].wait()
        start, stop = spans[h]

        def body(off, tile):
            lhs = h2[k % 2, :rows, :]
            for w, base in ((wg_v, 2 * start), (wu_v, start + stop)):
                weights = w[:, pl.ds(pl.multiple_of(start + off, 128), tile)]
                part[:, rows_of(k), pl.ds(pl.multiple_of(base + off, 128), tile)] = jnp.dot(lhs, weights, preferred_element_type=jnp.float32).astype(jnp.bfloat16).reshape(4, rb, tile)

        over_tiles(stop - start, 512, body)
        pair_first(k, h).start()
        pair_second(k, h).start()

    def pair_sum(k, h):
        pair_first(k, h).wait_recv()

        def body(off, tile):
            cols = pl.ds(pl.multiple_of(2 * spans[h][0] + off, 128), tile)
            cross_send[rows_of(k), cols] = (part[across, rows_of(k), cols].astype(jnp.float32) + pair_recv[0, rows_of(k), cols].astype(jnp.float32)).astype(jnp.bfloat16)

        over_tiles(2 * (spans[h][1] - spans[h][0]), 512, body)
        cross_copy(k, h).start()

    def activate(k, h):
        pair_second(k, h).wait_recv()
        cross_copy(k, h).wait_recv()
        start, stop = spans[h]

        def total(base, tile):
            cols = pl.ds(pl.multiple_of(base, 128), tile)
            return part[mx, rows_of(k), cols].astype(jnp.float32) + pair_recv[1, rows_of(k), cols].astype(jnp.float32) + cross_recv[rows_of(k), cols].astype(jnp.float32)

        def body(off, tile):
            gate = total(2 * start + off, tile)
            up = total(start + stop + off, tile)
            act[mx, rows_of(k), pl.ds(pl.multiple_of(start + off, 128), tile)] = (jax.nn.silu(gate) * up).astype(jnp.bfloat16)

        over_tiles(stop - start, 512, body)
        act_copy(k, h, 0).start()
        act_copy(k, h, 1).start()

    def forward_act(k, h):
        act_copy(k, h, 0).wait_recv()
        act_copy(k, h, 2).start()

    def down(k, h):
        rb = CHUNK_ROWS[k]
        rows = pl.ds(4 * CHUNK_STARTS[k], 4 * rb)
        act_copy(k, h, 1).wait_recv()
        act_copy(k, h, 2).wait_recv()
        if h == 0:
            if k == 0:
                loads[4].wait()
            acc[rows, :] = jnp.zeros((4 * rb, hid), jnp.float32)
        start, stop = spans[h]

        def body(off, tile):
            cols = pl.ds(pl.multiple_of(start + off, 128), tile)
            lhs = act[:, rows_of(k), cols].reshape(4 * rb, tile)
            acc[rows, :] += jnp.dot(lhs, wd_v[cols, :], preferred_element_type=jnp.float32)

        over_tiles(stop - start, 512, body)
        if h == len(spans) - 1:
            d_part[:, rows_of(k), :] = acc[rows, :].astype(jnp.bfloat16).reshape(4, rb, hid)
            for copy in reduce_copies(k, d_part, d_recv, s_red2, r_red2):
                copy.start()

    def out_block(k, h):
        for copy in reduce_copies(k, d_part, d_recv, s_red2, r_red2):
            copy.wait_recv()
        total = d_part[my, rows_of(k), :].astype(jnp.float32)
        for d in range(3):
            total += d_recv[d, rows_of(k), :].astype(jnp.float32)
        rows = pl.ds(pl.multiple_of(my * block + CHUNK_STARTS[k], 16), CHUNK_ROWS[k])
        out[rows, :] = (mid[my, rows_of(k), :].astype(jnp.float32) + total).astype(jnp.bfloat16)
        for copy in out_bcast(k):
            copy.start()

    def finish(k, h):
        for copy in out_bcast(k):
            copy.wait_recv()

    for load in first_loads:
        load.wait()
    for k in range(chunks):
        gather_to_across(k).start()
        gather_to_sib(k).start()
        attn_all[mx, rows_of(k), :] = attn[rows_of(k), :]
    stages = (forward_gather, out_proj, own_block, stats, gate_up, pair_sum, activate, forward_act, down, out_block, finish)
    for stage, k, h in PLAN:
        stages[stage](k, h)

    for k in range(chunks):
        sends = [gather_to_across(k), gather_to_sib(k), gather_forward(k)] + reduce_copies(k, o_part, o_recv, s_red, r_red) + bcast_copies(k, mid, s_bc, r_bc)
        sends += stat_copies(k) + reduce_copies(k, d_part, d_recv, s_red2, r_red2) + out_bcast(k)
        for h in range(len(spans)):
            sends += [pair_first(k, h), pair_second(k, h), cross_copy(k, h)] + [act_copy(k, h, which) for which in range(3)]
        for copy in sends:
            copy.wait_send()


def mlp_call(attn, x_in, gain, w_o, w_gate, w_up, w_down):
    row_total, hid = x_in.shape
    ff = w_gate.shape[1]
    block = row_total // 4
    chunks = len(CHUNK_ROWS)
    spans = len(SPAN_TILES)
    bf16 = jnp.bfloat16
    f32 = jnp.float32
    hbm = pl.BlockSpec(memory_space=pltpu.HBM)
    dma = pltpu.SemaphoreType.DMA
    four = pltpu.VMEM((4, block, hid), bf16)
    three = pltpu.VMEM((3, block, hid), bf16)
    return pl.pallas_call(
        mlp_kernel,
        out_shape=pltpu.VMEM((row_total, hid), bf16),
        in_specs=[hbm] * 7,
        out_specs=pl.BlockSpec(memory_space=pltpu.VMEM),
        scratch_shapes=[
            pltpu.VMEM(attn.shape, bf16), pltpu.VMEM((hid // 128, 128), bf16),
            pltpu.VMEM(w_o.shape, bf16), pltpu.VMEM(w_gate.shape, bf16), pltpu.VMEM(w_up.shape, bf16), pltpu.VMEM(w_down.shape, bf16),
            pltpu.VMEM((block, hid), bf16),
            four, four, three, four,
            pltpu.VMEM((chunks, 8, 128), f32), pltpu.VMEM((chunks, 3, 8, 128), f32),
            pltpu.VMEM((2, 4 * max(CHUNK_ROWS), hid), bf16),
            pltpu.VMEM((4, block, 2 * ff), bf16), pltpu.VMEM((2, block, 2 * ff), bf16),
            pltpu.VMEM((block, 2 * ff), bf16), pltpu.VMEM((block, 2 * ff), bf16),
            pltpu.VMEM((4, block, ff), bf16),
            pltpu.VMEM((4 * block, hid), f32),
            four, three,
            dma((7,)),
            dma((chunks, 3)), dma((chunks, 3)), dma((chunks, 3)), dma((chunks, 3)), dma((chunks, 3)), dma((chunks, 3)),
            dma((chunks, 3)), dma((chunks, 3)), dma((chunks, 2 * spans)), dma((chunks, 2 * spans)),
            dma((chunks, spans)), dma((chunks, spans)), dma((chunks, 3 * spans)), dma((chunks, 3 * spans)),
            dma((chunks, 3)), dma((chunks, 3)), dma((chunks, 3)), dma((chunks, 3)),
        ],
        compiler_params=pltpu.CompilerParams(collective_id=1, has_side_effects=True, vmem_limit_bytes=MLP_VMEM_BYTES),
        name="attn_out_mlp",
    )(*[in_hbm(a) for a in (attn, x_in, gain.reshape(-1, 128), w_o, w_gate, w_up, w_down)])


QKV_VMEM_BYTES = 9 * 1024 * 1024
ATTEND_VMEM_BYTES = 11 * 1024 * 1024


def qkv_kernel(x_hbm, seq_hbm, gain_hbm, w_q_hbm, w_k_hbm, w_v_hbm, b_q_hbm, b_k_hbm, b_v_hbm, k_cache, v_cache, q_out, k_out, v_out, k_held, v_held,
               x, seq, gain, w_q, w_k, w_v, b_q, b_k, b_v, load_sem, stat_send, stat_recv, h1, part, pair_recv, cross_send, cross_recv,
               s_stat, r_stat, s_pair, r_pair, s_cross, r_cross):
    mx, sib, across, across_sib = mx_peers()
    rows, hid = x.shape
    block = rows // 4
    q_cols = w_q.shape[1]
    loads = [pltpu.make_async_copy(src, dst, load_sem.at[i]) for i, (src, dst) in enumerate((
        (x_hbm, x), (gain_hbm, gain), (w_q_hbm, w_q), (w_k_hbm, w_k), (w_v_hbm, w_v), (b_q_hbm, b_q), (b_k_hbm, b_k), (b_v_hbm, b_v), (seq_hbm, seq)))]
    for load in loads:
        load.start()
    held = [pltpu.make_async_copy(src.at[pl.ds(0, dst.shape[0])], dst, load_sem.at[9 + i]) for i, (src, dst) in enumerate(((k_cache, k_held), (v_cache, v_held)))]
    for load in held:
        load.start()
    enter([("mx", sib), ("mx", across), ("mx", across_sib)])
    loads[0].wait()

    def remote(src, dst, send, recv, peer):
        return pltpu.make_async_remote_copy(src_ref=src, dst_ref=dst, send_sem=send, recv_sem=recv, device_id={"mx": peer}, device_id_type=MESH_IDS)

    for j in range(4):
        piece = x[j * block:(j + 1) * block].astype(jnp.float32)
        stat_send[:, j * block:(j + 1) * block] = column_to_lanes(jnp.sum(piece * piece, axis=1, keepdims=True))
    stat_copies = [remote(stat_send, stat_recv.at[d], s_stat.at[d], r_stat.at[d], p) for d, p in enumerate((sib, across, across_sib))]
    for copy in stat_copies:
        copy.start()
    for load in loads[1:]:
        load.wait()
    for copy in stat_copies:
        copy.wait_recv()
    total = stat_send[...] + stat_recv[0] + stat_recv[1] + stat_recv[2]
    stat_recv[0] = lax.rsqrt(total / (4 * hid) + NORM_EPS)
    gain_rows = gain[...].astype(jnp.float32)
    pair_copies = [remote(part.at[across_sib], pair_recv.at[0], s_pair.at[0], r_pair.at[0], sib),
                   remote(part.at[sib], pair_recv.at[1], s_pair.at[1], r_pair.at[1], sib)]
    cross = remote(cross_send, cross_recv, s_cross, r_cross, across)

    def project(j):
        start = pl.multiple_of(j * block, block)
        scale = lanes_to_column(stat_recv[0, :, pl.ds(start, block)])
        for t in range(hid // 128):
            cols = slice(t * 128, (t + 1) * 128)
            h1[:, cols] = (x[pl.ds(start, block), cols].astype(jnp.float32) * scale * gain_rows[t:t + 1]).astype(jnp.bfloat16)
        lhs = h1[...]
        off = 0
        for w in (w_q, w_k, w_v):
            part[j, :, off:off + w.shape[1]] = jnp.dot(lhs, w[...], preferred_element_type=jnp.float32).astype(jnp.bfloat16)
            off += w.shape[1]

    project(across_sib)
    pair_copies[0].start()
    project(across)
    pair_copies[0].wait_recv()
    cross_send[...] = (part[across].astype(jnp.float32) + pair_recv[0].astype(jnp.float32)).astype(jnp.bfloat16)
    cross.start()
    project(sib)
    pair_copies[1].start()
    project(mx)
    lane = lax.broadcasted_iota(jnp.int32, (block, HEAD), 1)
    inv_freq = jnp.exp(lax.rem(lane, HEAD // 2).astype(jnp.float32) * (-2.0 / HEAD * math.log(ROPE_THETA)))
    angles = lanes_to_column(seq[...].astype(jnp.float32)) * inv_freq
    cos_tab = jnp.cos(angles)
    sin_tab = jnp.where(lane < HEAD // 2, -jnp.sin(angles), jnp.sin(angles))
    pair_copies[1].wait_recv()
    cross.wait_recv()

    def total_of(off, bias):
        cols = slice(off, off + HEAD)
        return part[mx, :, cols].astype(jnp.float32) + pair_recv[1, :, cols].astype(jnp.float32) + cross_recv[:, cols].astype(jnp.float32) + bias.astype(jnp.float32)

    def rotated(vals):
        return (vals * cos_tab + pltpu.roll(vals, HEAD // 2, 1) * sin_tab).astype(jnp.bfloat16).astype(jnp.float32)

    heads = q_cols // HEAD
    for h in range(heads):
        q_out[:, h, :] = rotated(total_of(h * HEAD, b_q[h:h + 1]))
    for h in range(heads, q_out.shape[1]):
        q_out[:, h, :] = jnp.zeros((block, HEAD), jnp.float32)
    k_out[...] = rotated(total_of(q_cols, b_k[...]))
    v_out[...] = total_of(q_cols + HEAD, b_v[...]).astype(jnp.bfloat16).astype(jnp.float32)
    for copy in stat_copies + pair_copies + [cross]:
        copy.wait_send()
    for load in held:
        load.wait()


def qkv_call(x_in, seq_lens, gain, w_q, w_k, w_v, b_q, b_k, b_v, k_cache, v_cache):
    rows, hid = x_in.shape
    block = rows // 4
    cols = w_q.shape[1] + w_k.shape[1] + w_v.shape[1]
    held = pltpu.VMEM((HELD_ROWS,) + k_cache.shape[1:], jnp.bfloat16)
    heads_pad = -(-w_q.shape[1] // HEAD // 8) * 8
    bf16 = jnp.bfloat16
    f32 = jnp.float32
    vmem = pl.BlockSpec(memory_space=pltpu.VMEM)
    hbm = pl.BlockSpec(memory_space=pltpu.HBM)
    dma = pltpu.SemaphoreType.DMA
    return pl.pallas_call(
        qkv_kernel,
        out_shape=(pltpu.VMEM((block, heads_pad, HEAD), f32), pltpu.VMEM((block, HEAD), f32), pltpu.VMEM((block, HEAD), f32), held, held),
        in_specs=[hbm] * 11,
        out_specs=(vmem,) * 5,
        scratch_shapes=[
            pltpu.VMEM(x_in.shape, bf16), pltpu.VMEM((1, block), jnp.int32), pltpu.VMEM((hid // 128, 128), bf16),
            pltpu.VMEM(w_q.shape, bf16), pltpu.VMEM(w_k.shape, bf16), pltpu.VMEM(w_v.shape, bf16),
            pltpu.VMEM((w_q.shape[1] // HEAD, HEAD), bf16), pltpu.VMEM((1, HEAD), bf16), pltpu.VMEM((1, HEAD), bf16), dma((11,)),
            pltpu.VMEM((8, rows), f32), pltpu.VMEM((3, 8, rows), f32), pltpu.VMEM((block, hid), bf16),
            pltpu.VMEM((4, block, cols), bf16), pltpu.VMEM((2, block, cols), bf16), pltpu.VMEM((block, cols), bf16), pltpu.VMEM((block, cols), bf16),
            dma((3,)), dma((3,)), dma((2,)), dma((2,)), dma, dma,
        ],
        compiler_params=pltpu.CompilerParams(collective_id=0, has_side_effects=True, vmem_limit_bytes=QKV_VMEM_BYTES),
        name="norm_qkv",
    )(*[in_hbm(a) for a in (x_in, seq_lens.reshape(1, block), gain.reshape(-1, 128), w_q, w_k, w_v, b_q.reshape(-1, HEAD), b_k.reshape(1, -1), b_v.reshape(1, -1), k_cache, v_cache)])


HELD_ROWS = 96
GROUP_ROWS = 4
SLOTS = 8


def attend_kernel(seq_hbm, q, k_new, v_new, k_held, v_held, k_cache, v_cache, attn_hbm, k_out, v_out, k_buf, v_buf, heads_out, attn, seq, in_sem, out_sem, held_sem, misc_sem):
    batch, length, _ = k_cache.shape
    held_groups = HELD_ROWS // GROUP_ROWS
    fetched = (batch - HELD_ROWS) // GROUP_ROWS
    seq_load = pltpu.make_async_copy(seq_hbm, seq, misc_sem.at[0])
    seq_load.start()

    def rows_of(i):
        return pl.ds(i * GROUP_ROWS, GROUP_ROWS)

    def fetch(i):
        slot = lax.rem(i, SLOTS)
        return (pltpu.make_async_copy(k_cache.at[rows_of(i + held_groups)], k_buf.at[slot], in_sem.at[0, slot]),
                pltpu.make_async_copy(v_cache.at[rows_of(i + held_groups)], v_buf.at[slot], in_sem.at[1, slot]))

    def flush(i):
        slot = lax.rem(i, SLOTS)
        return (pltpu.make_async_copy(k_buf.at[slot], k_out.at[rows_of(i + held_groups)], out_sem.at[0, slot]),
                pltpu.make_async_copy(v_buf.at[slot], v_out.at[rows_of(i + held_groups)], out_sem.at[1, slot]))

    def flush_held(i):
        return (pltpu.make_async_copy(k_held.at[rows_of(i)], k_out.at[rows_of(i)], held_sem.at[0]),
                pltpu.make_async_copy(v_held.at[rows_of(i)], v_out.at[rows_of(i)], held_sem.at[1]))

    def attend(first, k_group, v_group):
        tile_row = lax.broadcasted_iota(jnp.int32, (16, HEAD), 0)
        for r in range(GROUP_ROWS):
            b = first + r
            pos = seq[b]
            base = pl.multiple_of(pos // 16 * 16, 16)
            hit = tile_row == pos - base
            for group, new in ((k_group, k_new), (v_group, v_new)):
                tile = group[r, pl.ds(base, 16), :].astype(jnp.float32)
                group[r, pl.ds(base, 16), :] = jnp.where(hit, new[pl.ds(b, 1), :], tile).astype(jnp.bfloat16)
        scores = []
        for r in range(GROUP_ROWS):
            b = first + r
            s = lax.dot_general(q[b].astype(jnp.bfloat16), k_group[r], (((1,), (1,)), ((), ())), preferred_element_type=jnp.float32) * HEAD ** -0.5
            t = lax.broadcasted_iota(jnp.int32, s.shape, 1)
            scores.append(jnp.where(t <= seq[b], s, -jnp.inf))
        for r in range(GROUP_ROWS):
            s = scores[r]
            w = jnp.exp(s - jnp.max(s, axis=1, keepdims=True))
            total = jnp.sum(w, axis=1, keepdims=True)
            o = jnp.dot(w.astype(jnp.bfloat16), v_group[r], preferred_element_type=jnp.float32)
            heads_out[first + r] = o / total

    for i in range(SLOTS):
        for copy in fetch(jnp.int32(i)):
            copy.start()
    seq_load.wait()

    def held_step(i, carry):
        attend(i * GROUP_ROWS, k_held.at[rows_of(i)], v_held.at[rows_of(i)])
        for copy in flush_held(i):
            copy.start()
        return carry

    def fetched_step(i, carry):
        slot = lax.rem(i, SLOTS)
        for copy in fetch(i):
            copy.wait()
        attend((i + held_groups) * GROUP_ROWS, k_buf.at[slot], v_buf.at[slot])
        for copy in flush(i):
            copy.start()
        return carry

    lax.fori_loop(0, held_groups, held_step, 0)
    lax.fori_loop(0, fetched, fetched_step, 0)
    for h in range(attn.shape[1] // HEAD):
        attn[:, h * HEAD:(h + 1) * HEAD] = heads_out[:, h, :].astype(jnp.bfloat16)
    attn_store = pltpu.make_async_copy(attn, attn_hbm, misc_sem.at[1])
    attn_store.start()
    for src, dst, sem in ((k_held, k_out, held_sem.at[0]), (v_held, v_out, held_sem.at[1])):
        pltpu.make_async_copy(src, dst.at[pl.ds(0, HELD_ROWS)], sem).wait()
    for i in range(fetched):
        for copy in flush(jnp.int32(i)):
            copy.wait()
    attn_store.wait()


def attend_call(seq_lens, q, k_new, v_new, k_held, v_held, k_cache, v_cache, q_cols):
    batch, length, _ = k_cache.shape
    bf16 = jnp.bfloat16
    f32 = jnp.float32
    vmem = pl.BlockSpec(memory_space=pltpu.VMEM)
    hbm = pl.BlockSpec(memory_space=pltpu.HBM)
    dma = pltpu.SemaphoreType.DMA
    return pl.pallas_call(
        attend_kernel,
        out_shape=(pltpu.HBM((batch, q_cols), bf16), jax.ShapeDtypeStruct(k_cache.shape, bf16), jax.ShapeDtypeStruct(k_cache.shape, bf16)),
        in_specs=[hbm] + [vmem] * 5 + [hbm] * 2,
        out_specs=(hbm, hbm, hbm),
        scratch_shapes=[
            pltpu.VMEM((SLOTS, GROUP_ROWS, length, HEAD), bf16), pltpu.VMEM((SLOTS, GROUP_ROWS, length, HEAD), bf16),
            pltpu.VMEM(q.shape, f32), pltpu.VMEM((batch, q_cols), bf16), pltpu.SMEM((batch,), jnp.int32),
            dma((2, SLOTS)), dma((2, SLOTS)), dma((2,)), dma((2,)),
        ],
        compiler_params=pltpu.CompilerParams(vmem_limit_bytes=ATTEND_VMEM_BYTES),
        name="attend_and_update",
    )(in_hbm(seq_lens), *[in_vmem(a) for a in (q, k_new, v_new, k_held, v_held)], in_hbm(k_cache), in_hbm(v_cache))


def solution(mesh):
    act_spec = P(None, "mx")
    cache_spec = P("mx", None, "my", None)
    in_specs = (act_spec, P("mx"), P("mx"), P("mx"), P("mx", "my"), P("my"), P("mx", "my"), P("my"), P("mx", "my"), P("my"), P("my", "mx"), P("mx", "my"), P("mx", "my"), P("my", "mx"), cache_spec, cache_spec)
    out_specs = (act_spec, cache_spec, cache_spec)

    def local_layer(x_in, seq_lens, gain_attn, gain_mlp, w_q, b_q, w_k, b_k, w_v, b_v, w_o, w_gate, w_up, w_down, k_cache, v_cache):
        k_flat = k_cache.reshape(k_cache.shape[:2] + (HEAD,))
        v_flat = v_cache.reshape(k_flat.shape)
        q, k_new, v_new, k_held, v_held = qkv_call(x_in, seq_lens, gain_attn, w_q, w_k, w_v, b_q, b_k, b_v, k_flat, v_flat)
        attn, k_out, v_out = attend_call(seq_lens, q, k_new, v_new, k_held, v_held, k_flat, v_flat, w_q.shape[1])
        x_out = mlp_call(attn, x_in, gain_mlp, w_o, w_gate, w_up, w_down)
        return x_out, k_out.reshape(k_cache.shape), v_out.reshape(v_cache.shape)

    return jax.shard_map(local_layer, mesh=mesh, in_specs=in_specs, out_specs=out_specs, check_vma=False)
```

time: 177 us -> 157 us (0.89)
  Pallas kernels: 174 us -> 156 us
    pallas_call x3, Pallas kernels: 174 us -> 156 us  [the longest x1 120 us: mlp_call(): pl.pallas_call(mlp_kernel, out_shape=pltpu.VMEM((row_total, hid), bf16),...]
where the time goes in v3:
time: 157 us
  Pallas kernels  156 us (99%)
    pallas_call x1, Pallas kernels, mlp_call(): pl.pallas_call(mlp_kernel, out_shape=pltpu.VMEM((row_total, hid), bf16),...  120 us
    pallas_call x1, Pallas kernels, attend_call(): pl.pallas_call(attend_kernel, out_shape=(pltpu.HBM((batch, q_cols), bf16)...  17.8 us
    pallas_call x1, Pallas kernels, qkv_call(): pl.pallas_call(qkv_kernel, out_shape=(pltpu.VMEM((block, heads_pad, HEAD)...  17.5 us

profile of v3, /device:TPU:0, one launch (start us, length us, event | category | flops | bytes accessed | tf_op | source)
XLA Modules:
  0.0 157.3 jit_solution(11359806633020174082)
XLA Ops:
  0.6 17.5 %norm_qkv.1 = (f32[128,8,128]{2,1,0:T(8,128)S(1)}, f32[128,128]{1,0:T(8,128)S(1)}, f32[128,128]{1,0:T(8,128)S(1)}, bf16[96,512,128]{2,1,0:T(8,128)(2,1)S(1)}, bf16[96,512,128]{2,1,0:T(8,128)(2,1)S(1)}) custom-call(bf16[512,896]{1,0:T(8,128)(2,1)} %x_in.1, s32[1,128]{1,0:T(1,128)} %bitcast.21, bf16[7,128]{1,0:T(8,128)(2,1)} %bitcast.19, ...), custom_call_target="tpu_custom_call" | custom-call | tf_op jit(solution)/shard_map/norm_qkv/pallas_call | solution.py:441
  18.2 17.8 %attend_and_update.1 = (bf16[128,896]{1,0:T(8,128)(2,1)}, bf16[128,512,128]{2,1,0:T(8,128)(2,1)}, bf16[128,512,128]{2,1,0:T(8,128)(2,1)}) custom-call(s32[128]{0:T(128)} %seq_hbm.1, f32[128,8,128]{2,1,0:T(8,128)S(1)} %get-tuple-element.11.q, f32[128,128]{1,0:T(8,128)S(1)} %get-tuple-element.12.k_new, f32[128,128]{1,0:T(8,128)S(1)} %get-tuple-element.13.v_new, ...), custom_call_target="tpu_custom_call" | custom-call | tf_op jit(solution)/shard_map/attend_and_update/pallas_call | solution.py:552
  36.0 120.3 %attn_out_mlp.1 = bf16[512,896]{1,0:T(8,128)(2,1)S(1)} custom-call(bf16[128,896]{1,0:T(8,128)(2,1)} %get-tuple-element.16.attn_hbm, bf16[512,896]{1,0:T(8,128)(2,1)} %x_in.1, bf16[7,128]{1,0:T(8,128)(2,1)} %bitcast.18, bf16[896,896]{1,0:T(8,128)(2,1)} %w_o.1, bf16[896,4736]{1,0:T(8,128)(2,1)} %w_gate.1, bf16[896,4736]{1,0:T(8,128)(2,1)} %w_up.1, ...), custom_call_target="tpu_custom_call" | custom-call | tf_op jit(solution)/shard_map/attn_out_mlp/pallas_call | solution.py:312
  156.4 0.9 copy.22
